TPU v7x, 32 devices: a 4x4x1 block of a 4x4x8 slice. The times are simulated.
32 devices in a mesh: dp: 1 (over z), ep: 32 (over y, x, core).
Axes of the slice: x: 4, y: 4, z: 1, core: 2. Of those that a mesh axis runs over, the one named last changes fastest.
The devices are a block of a 4x4x8 slice.
Arguments:
- x_disp: bfloat16 [32, 64, 48, 1536], P('dp', 'ep')
- w_gate: bfloat16 [64, 1536, 512], P('ep')
- w_up: bfloat16 [64, 1536, 512], P('ep')
- w_down: bfloat16 [64, 512, 1536], P('ep')
- d_out: bfloat16 [8192, 1536], P(('dp', 'ep'))
- slot_idx: int32 [8192, 6], P(('dp', 'ep'))
- expert_id: int32 [8192, 6], P(('dp', 'ep'))
- gate_wt: float32 [8192, 6], P(('dp', 'ep'))
Outputs:
- output 1: bfloat16 [32, 64, 48, 1536], P('dp', 'ep')
- output 2: bfloat16 [64, 1536, 512], P(('dp', 'ep'))
- output 3: bfloat16 [64, 1536, 512], P(('dp', 'ep'))
- output 4: bfloat16 [64, 512, 1536], P(('dp', 'ep'))
- output 5: float32 [8192, 6], P(('dp', 'ep'))
All inputs are finite; a program needn't handle non-finite values.
Results may differ from a plain program's by a relative error of at most 0.001.
Values are sent between devices in bfloat16 or wider.
A program may use at most 768 MiB of HBM per device.

v0:
```python
import jax
import jax.numpy as jnp
from jax import lax
from jax.sharding import PartitionSpec as P


def expert_backward(x_rows, out_rows, gate_rows, w_gate, w_up, w_down):
    d_slot = (out_rows.astype(jnp.float32) * gate_rows[..., None]).astype(jnp.bfloat16)
    pre_gate = jnp.einsum('secd,edf->secf', x_rows, w_gate, preferred_element_type=jnp.float32)
    pre_up = jnp.einsum('secd,edf->secf', x_rows, w_up, preferred_element_type=jnp.float32)
    gate_sig = jax.nn.sigmoid(pre_gate)
    silu_gate = pre_gate * gate_sig
    hidden = (silu_gate * pre_up).astype(jnp.bfloat16)
    y_rows = jnp.einsum('secf,efd->secd', hidden, w_down, preferred_element_type=jnp.float32).astype(jnp.bfloat16)
    grad_hidden = jnp.einsum('secd,efd->secf', d_slot, w_down, preferred_element_type=jnp.float32).astype(jnp.bfloat16).astype(jnp.float32)
    grad_pre_gate = (grad_hidden * pre_up * gate_sig * (1.0 + pre_gate * (1.0 - gate_sig))).astype(jnp.bfloat16)
    grad_pre_up = (grad_hidden * silu_gate).astype(jnp.bfloat16)
    grad_x = (jnp.einsum('secf,edf->secd', grad_pre_gate, w_gate, preferred_element_type=jnp.float32) + jnp.einsum('secf,edf->secd', grad_pre_up, w_up, preferred_element_type=jnp.float32)).astype(jnp.bfloat16)
    grad_w_gate = jnp.einsum('secd,secf->edf', x_rows, grad_pre_gate, preferred_element_type=jnp.float32).astype(jnp.bfloat16)
    grad_w_up = jnp.einsum('secd,secf->edf', x_rows, grad_pre_up, preferred_element_type=jnp.float32).astype(jnp.bfloat16)
    grad_w_down = jnp.einsum('secf,secd->efd', hidden, d_slot, preferred_element_type=jnp.float32).astype(jnp.bfloat16)
    gate_grad_rows = jnp.einsum('secd,secd->sec', out_rows, y_rows, preferred_element_type=jnp.float32)
    return grad_x, grad_w_gate, grad_w_up, grad_w_down, gate_grad_rows


def solution(mesh):
    group_size = mesh.shape['ep']

    def local_step(x_disp, w_gate, w_up, w_down, d_out, slot_idx, expert_id, gate_wt):
        e_local, capacity, model_dim = x_disp.shape[1], x_disp.shape[2], x_disp.shape[3]
        tok_dev, top_k = slot_idx.shape
        slot_count = group_size * e_local * capacity
        flat_pos = jnp.where(slot_idx >= 0, expert_id * capacity + slot_idx, slot_count)
        choice_ids = jnp.arange(tok_dev * top_k, dtype=jnp.int32)
        owner_ids = jnp.full((slot_count,), tok_dev * top_k, jnp.int32).at[flat_pos.reshape(-1)].set(choice_ids, mode='drop')
        send_rows = jnp.take(d_out, owner_ids // top_k, axis=0, mode='fill', fill_value=0).reshape(group_size, e_local, capacity, model_dim)
        send_gates = jnp.take(gate_wt.reshape(-1), owner_ids, mode='fill', fill_value=0).reshape(group_size, e_local, capacity)
        out_rows = lax.all_to_all(send_rows, 'ep', 0, 0, tiled=True)
        gate_rows = lax.all_to_all(send_gates, 'ep', 0, 0, tiled=True)
        grad_x, grad_w_gate, grad_w_up, grad_w_down, gate_grad_rows = expert_backward(x_disp, out_rows, gate_rows, w_gate, w_up, w_down)
        back_rows = lax.all_to_all(gate_grad_rows, 'ep', 0, 0, tiled=True)
        grad_gate = jnp.take(back_rows.reshape(-1), flat_pos, mode='fill', fill_value=0)
        return grad_x, grad_w_gate, grad_w_up, grad_w_down, grad_gate

    token_place = P(('dp', 'ep'), None)
    weight_place = P('ep', None, None)
    slot_place = P('dp', 'ep', None, None)
    grad_place = P(('dp', 'ep'), None, None)
    return jax.shard_map(local_step, mesh=mesh,
                         in_specs=(slot_place, weight_place, weight_place, weight_place, token_place, token_place, token_place, token_place),
                         out_specs=(slot_place, grad_place, grad_place, grad_place, token_place),
                         check_vma=False)
```

profile of v0, /device:TPU:97, one launch (start us, length us, event | category | flops | bytes accessed | tf_op | source)
XLA Modules:
  0.0 319.2 jit_solution(4166366639567196393)
XLA Ops:
  0.6 0.0 copy-start
  0.6 0.9 compare_select_fusion.3
  1.5 0.0 copy-start.2
  1.5 0.1 copy.54
  1.7 0.1 reshape.75
  1.9 6.2 %scatter_custom_fusion = s32[3072]{0:T(1024)S(1)} fusion(s32[1536]{0:T(1024)S(1)} %fusion.48, s32[1536]{0:T(1024)S(1)} %iota.3, s32[]{:T(128)} %constant.36.clone.1), kind=kCustom, calls=%fused_computation.65 | custom fusion | bytes 12292 | tf_op jit(solution)/shard_map/scatter | solution.py:35
  8.1 0.0 copy-done.2
  8.1 0.8 copy.55
  8.9 0.1 reshape.76
  9.1 17.4 %gather_fusion.1 = f32[3072]{0:T(1024)S(1)} fusion(f32[1536]{0:T(1024)S(1)} %reshape.76, s32[3072]{0:T(1024)S(1)} %get-tuple-element.30), kind=kCustom, calls=%fused_computation.1 | custom fusion | bytes 36864 | tf_op jit(solution)/shard_map/jit(_take)/gather | solution.py:37
  26.5 0.7 select_n.56
  27.2 9.1 %all-to-all-start.1 = ((f32[32,2,48]{2,1,0:T(2,128)}), f32[32,2,48]{2,1,0:T(2,128)S(1)}, u32[]{:S(2)}, u32[]{:S(2)}) async-start(f32[32,2,48]{2,1,0:T(2,128)} %select_n.56), calls=%async_computation.1 | async-start | bytes 65536 | tf_op jit(solution)/shard_map/all_to_all | solution.py:39
  36.4 0.1 broadcast_in_dim.41
  36.5 20.5 %gather_fusion = bf16[3072,1536]{1,0:T(8,128)(2,1)} fusion(bf16[256,1536]{1,0:T(8,128)(2,1)} %param.12, s32[3072]{0:T(1024)S(1)} %get-tuple-element.29), kind=kCustom, calls=%fused_computation | custom fusion | bytes 18886656 | tf_op jit(solution)/shard_map/jit(_take)/gather | solution.py:36
  57.0 8.2 %broadcast_select_fusion = bf16[32,2,48,1536]{3,2,1,0:T(8,128)(2,1)} fusion(bf16[32,2,48,1536]{3,2,1,0:T(8,128)(2,1)} %bitcast.94, pred[32,2,48]{2,1,0:T(4,128)(4,1)S(1)} %broadcast_in_dim.41), kind=kLoop, calls=%fused_computation.8 | loop fusion | flops 4718592 | bytes 18877440 | tf_op jit(solution)/shard_map/jit(_take)/select_n | solution.py:36
  65.1 0.0 all-to-all-done.1
  65.2 6.3 %all-to-all-start = ((bf16[32,2,48,1536]{3,2,1,0:T(8,128)(2,1)}), bf16[32,2,48,1536]{3,2,1,0:T(8,128)(2,1)}, u32[]{:S(2)}, u32[]{:S(2)}) async-start(bf16[32,2,48,1536]{3,2,1,0:T(8,128)(2,1)} %broadcast_select_fusion), calls=%async_computation | async-start | bytes 18874368 | tf_op jit(solution)/shard_map/all_to_all | solution.py:38
  71.5 0.1 copy.62
  71.6 0.1 reshape.96
  71.8 0.6 pad_clamp_fusion
  72.4 11.2 %fusion.18 = f32[2,512,32,48]{1,3,2,0:T(8,128)} fusion(bf16[32,2,48,1536]{3,2,1,0:T(8,128)(2,1)} %param.8, bf16[2,1536,512]{2,1,0:T(8,128)(2,1)} %param.9), kind=kOutput, calls=%fused_computation.35 | convolution fusion | flops 4831838208 | bytes 18874368 | tf_op jit(solution)/shard_map/secd,edf->secf/dot_general | solution.py:9
  83.6 105.9 %all-to-all-done = bf16[32,2,48,1536]{3,2,1,0:T(8,128)(2,1)} async-done(((bf16[32,2,48,1536]{3,2,1,0:T(8,128)(2,1)}), bf16[32,2,48,1536]{3,2,1,0:T(8,128)(2,1)}, u32[]{:S(2)}, u32[]{:S(2)}) %all-to-all-start) | async-done | bytes 9437216 | tf_op jit(solution)/shard_map/all_to_all | solution.py:38
  189.5 9.8 %fusion.41 = bf16[2,32,48,512]{3,2,1,0:T(8,128)(2,1)} fusion(bf16[2,512,1536]{2,1,0:T(8,128)(2,1)} %param.11, f32[32,2,48]{2,1,0:T(2,128)S(1)} %all-to-all-done.1, bf16[32,2,48,1536]{3,2,1,0:T(8,128)(2,1)} %all-to-all-done), kind=kOutput, calls=%fused_computation.48 | convolution fusion | flops 4847566848 | bytes 15740928 | tf_op jit(solution)/shard_map/secd,efd->secf/dot_general | solution.py:15
  199.3 13.6 %fusion.31 = bf16[2,1536,512]{1,2,0:T(8,128)(2,1)} fusion(bf16[32,2,48,1536]{3,2,1,0:T(8,128)(2,1)} %param.8, bf16[2,32,48,512]{3,2,1,0:T(8,128)(2,1)} %fusion.41, f32[2,512,32,48]{1,3,2,0:T(8,128)} %fusion.18), kind=kOutput, calls=%fused_computation.40 | convolution fusion | flops 4844421120 | bytes 22020096 | tf_op jit(solution)/shard_map/secd,secf->edf/dot_general | solution.py:20
  212.9 0.0 copy-done
  212.9 12.5 %fusion.12 = (bf16[32,2,48,512]{3,2,0,1:T(8,128)(2,1)}, bf16[32,2,48,512]{3,2,0,1:T(8,128)(2,1)S(1)}) fusion(f32[2,512,32,48]{1,3,2,0:T(8,128)} %fusion.18, bf16[2,32,48,512]{3,2,1,0:T(8,128)(2,1)} %fusion.41, bf16[32,2,48,1536]{3,2,1,0:T(8,128)(2,1)} %param.8, bf16[2,1536,512]{2,1,0:T(8,128)(2,1)S(1)} %copy-done), kind=kOutput, calls=%fused_computation.28 | convolution fusion | flops 4853858304 | bytes 28311552 | tf_op jit(solution)/shard_map/secd,edf->secf/dot_general | solution.py:10
  225.4 0.0 copy-start.4
  225.4 10.3 %fusion.28 = bf16[2,1536,512]{1,2,0:T(8,128)(2,1)} fusion(bf16[32,2,48,512]{3,2,0,1:T(8,128)(2,1)S(1)} %get-tuple-element.28, bf16[32,2,48,1536]{3,2,1,0:T(8,128)(2,1)} %param.8), kind=kOutput, calls=%fused_computation.39 | convolution fusion | flops 4833411072 | bytes 15728640 | tf_op jit(solution)/shard_map/secd,secf->edf/dot_general | solution.py:19
  235.7 0.0 copy-done.4
  235.7 0.0 copy-start.5
  235.7 0.0 copy-start.6
  235.7 9.2 %fusion.34 = f32[2,32,48,1536]{3,2,1,0:T(8,128)} fusion(bf16[32,2,48,512]{3,2,0,1:T(8,128)(2,1)S(1)} %get-tuple-element.28, bf16[2,1536,512]{2,1,0:T(8,128)(2,1)S(1)} %copy-done.4), kind=kOutput, calls=%fused_computation.41 | convolution fusion | flops 4831838208 | bytes 25165824 | tf_op jit(solution)/shard_map/secf,edf->secd/dot_general | solution.py:18
  244.9 0.0 copy-done.5
  244.9 0.0 copy-done.6
  244.9 8.0 %multiply_reduce_fusion = f32[32,2,48]{2,0,1:T(8,128)S(1)} fusion(bf16[32,2,48,512]{3,2,0,1:T(8,128)(2,1)S(1)} %copy-done.6, bf16[2,512,1536]{2,1,0:T(8,128)(2,1)S(1)} %copy-done.5, bf16[32,2,48,1536]{3,2,1,0:T(8,128)(2,1)} %all-to-all-done), kind=kOutput, calls=%fused_computation.4 | convolution fusion | flops 4855428096 | bytes 15740928 | tf_op jit(solution)/shard_map/secf,efd->secd/dot_general | solution.py:14
  252.8 0.6 copy.77
  253.5 13.8 %all-to-all-start.2 = ((f32[32,2,48]{2,1,0:T(2,128)}), f32[32,2,48]{2,1,0:T(2,128)S(1)}, u32[]{:S(2)}, u32[]{:S(2)}) async-start(f32[32,2,48]{2,1,0:T(2,128)} %copy.77), calls=%async_computation.2 | async-start | bytes 65536 | tf_op jit(solution)/shard_map/all_to_all | solution.py:41
  267.3 9.8 %bitcast_convert_fusion = bf16[2,512,1536]{2,1,0:T(8,128)(2,1)} fusion(bf16[32,2,48,512]{3,2,0,1:T(8,128)(2,1)} %get-tuple-element.27, f32[32,2,48]{2,1,0:T(2,128)S(1)} %all-to-all-done.1, bf16[32,2,48,1536]{3,2,1,0:T(8,128)(2,1)} %all-to-all-done), kind=kOutput, calls=%fused_computation.13 | convolution fusion | flops 4847566848 | bytes 15740928 | tf_op jit(solution)/shard_map/secf,secd->efd/dot_general | solution.py:21
  277.1 15.1 %fusion = bf16[32,2,48,1536]{3,2,0,1:T(8,128)(2,1)} fusion(f32[2,32,48,1536]{3,2,1,0:T(8,128)} %fusion.34, bf16[2,1536,512]{2,1,0:T(8,128)(2,1)S(1)} %copy-done, bf16[2,32,48,512]{3,2,1,0:T(8,128)(2,1)} %fusion.41, f32[2,512,32,48]{1,3,2,0:T(8,128)} %fusion.18), kind=kOutput, calls=%fused_computation.7 | convolution fusion | flops 4852285440 | bytes 40894464 | tf_op jit(solution)/shard_map/secf,edf->secd/dot_general | solution.py:18
  292.2 4.6 %copy.66 = bf16[2,1536,512]{2,1,0:T(8,128)(2,1)} copy(bf16[2,1536,512]{1,2,0:T(8,128)(2,1)} %fusion.31) | data formatting | bytes 6291456
  296.9 4.6 %copy.65 = bf16[2,1536,512]{2,1,0:T(8,128)(2,1)} copy(bf16[2,1536,512]{1,2,0:T(8,128)(2,1)} %fusion.28) | data formatting | bytes 6291456
  301.5 0.0 copy-start.1
  301.5 8.4 %copy.64 = bf16[32,2,48,1536]{3,2,1,0:T(8,128)(2,1)} copy(bf16[32,2,48,1536]{3,2,0,1:T(8,128)(2,1)} %fusion) | data formatting | bytes 18874368
  309.9 0.0 all-to-all-done.2
  309.9 0.1 reshape.77
  310.0 0.0 copy-done.1
  310.0 0.0 copy-start.3
  310.0 8.4 %gather_fusion.2 = f32[1536]{0:T(1024)S(1)} fusion(f32[3072]{0:T(1024)S(1)} %reshape.77, s32[2048]{0:T(1024)S(1)} %copy-done.1), kind=kCustom, calls=%fused_computation.2 | custom fusion | bytes 18432 | tf_op jit(solution)/shard_map/jit(_take)/gather | solution.py:42
  318.4 0.1 reshape.95
  318.5 0.1 copy.63
  318.6 0.0 copy-done.3
  318.6 0.6 and_select_fusion.1
  (5 shorter events, 0.1 us)
Async XLA Ops:
  0.6 212.2 %copy-start = (bf16[2,1536,512]{2,1,0:T(8,128)(2,1)S(1)}, bf16[2,1536,512]{2,1,0:T(8,128)(2,1)}, u32[]{:S(2)}) copy-start(bf16[2,1536,512]{2,1,0:T(8,128)(2,1)} %param.10) | copy-start | bytes 9437188
  1.5 6.5 %copy-start.2 = (s32[256,6]{0,1:T(8,128)}, s32[256,6]{0,1:T(8,128)S(1)}, u32[]{:S(2)}) copy-start(s32[256,6]{0,1:T(8,128)S(1)} %get-tuple-element.26) | copy-start | bytes 18436
  27.2 37.9 %all-to-all-start.1 = ((f32[32,2,48]{2,1,0:T(2,128)}), f32[32,2,48]{2,1,0:T(2,128)S(1)}, u32[]{:S(2)}, u32[]{:S(2)}) async-start(f32[32,2,48]{2,1,0:T(2,128)} %select_n.56), calls=%async_computation.1 | async-start | bytes 65536 | tf_op jit(solution)/shard_map/all_to_all | solution.py:39
  65.2 124.4 %all-to-all-start = ((bf16[32,2,48,1536]{3,2,1,0:T(8,128)(2,1)}), bf16[32,2,48,1536]{3,2,1,0:T(8,128)(2,1)}, u32[]{:S(2)}, u32[]{:S(2)}) async-start(bf16[32,2,48,1536]{3,2,1,0:T(8,128)(2,1)} %broadcast_select_fusion), calls=%async_computation | async-start | bytes 18874368 | tf_op jit(solution)/shard_map/all_to_all | solution.py:38
  225.4 10.3 %copy-start.4 = (bf16[2,1536,512]{2,1,0:T(8,128)(2,1)S(1)}, bf16[2,1536,512]{2,1,0:T(8,128)(2,1)}, u32[]{:S(2)}) copy-start(bf16[2,1536,512]{2,1,0:T(8,128)(2,1)} %param.9) | copy-start | bytes 9437188
  235.7 9.2 %copy-start.5 = (bf16[2,512,1536]{2,1,0:T(8,128)(2,1)S(1)}, bf16[2,512,1536]{2,1,0:T(8,128)(2,1)}, u32[]{:S(2)}) copy-start(bf16[2,512,1536]{2,1,0:T(8,128)(2,1)} %param.11) | copy-start | bytes 9437188
  235.7 9.2 %copy-start.6 = (bf16[32,2,48,512]{3,2,0,1:T(8,128)(2,1)S(1)}, bf16[32,2,48,512]{3,2,0,1:T(8,128)(2,1)}, u32[]{:S(2)}) copy-start(bf16[32,2,48,512]{3,2,0,1:T(8,128)(2,1)} %get-tuple-element.27) | copy-start | bytes 9437188
  253.5 56.4 %all-to-all-start.2 = ((f32[32,2,48]{2,1,0:T(2,128)}), f32[32,2,48]{2,1,0:T(2,128)S(1)}, u32[]{:S(2)}, u32[]{:S(2)}) async-start(f32[32,2,48]{2,1,0:T(2,128)} %copy.77), calls=%async_computation.2 | async-start | bytes 65536 | tf_op jit(solution)/shard_map/all_to_all | solution.py:41
  301.5 8.5 %copy-start.1 = (s32[2048]{0:T(1024)S(1)}, s32[2048]{0:T(1024)}, u32[]{:S(2)}) copy-start(s32[2048]{0:T(1024)} %pad_clamp_fusion) | copy-start | bytes 24580
  310.0 8.6 %copy-start.3 = (s32[256,6]{0,1:T(8,128)S(1)}, s32[256,6]{0,1:T(8,128)}, u32[]{:S(2)}) copy-start(s32[256,6]{0,1:T(8,128)} %copy-done.2) | copy-start | bytes 18436
where the time goes:
time: 320 us; the launch traced here: 319 us
  waiting for transfers between devices  106 us (33%)
  matrix products  99.5 us (31%)
  local copies, waits for them, and re-layouts  73.4 us (23%)
  starting transfers between devices  29.3 us (9%)
  other arithmetic  10.3 us (3%)
    all_to_all x1, waiting for transfers between devices, local_step(): out_rows = lax.all_to_all(send_rows, 'ep', 0, 0, tiled=True)  106 us
    gather x1, local copies, waits for them, and re-layouts, local_step(): jnp.take(d_out, owner_ids // top_k, axis=0, mode='fill', fill_value=0)  20.5 us
    unnamed x18, local copies, waits for them, and re-layouts  18.5 us
    gather x1, local copies, waits for them, and re-layouts, local_step(): jnp.take(gate_wt.reshape(-1), owner_ids, mode='fill', fill_value=0)  17.4 us
    dot_general x1, matrix products, expert_backward(): jnp.einsum('secf,edf->secd', grad_pre_up, w_up, preferred_element_type=jn...  15.1 us
    all_to_all x1, starting transfers between devices, local_step(): back_rows = lax.all_to_all(gate_grad_rows, 'ep', 0, 0, tiled=True)  13.8 us
    dot_general x1, matrix products, expert_backward(): jnp.einsum('secd,secf->edf', x_rows, grad_pre_up, preferred_element_type=...  13.6 us
    dot_general x1, matrix products, expert_backward(): jnp.einsum('secd,edf->secf', x_rows, w_up, preferred_element_type=jnp.flo...  12.5 us
  transfers between devices with their start and end apart: 3, of which 1 were waited for; matrix products, arithmetic and copies ran while one was open for 26% of the time, Pallas kernels for 0%

commit v1 on v0

v1 whole, which is shorter than its diff:
```python
import functools
import math

import jax
import jax.numpy as jnp
from jax import lax
from jax.experimental import pallas as pl
from jax.experimental.pallas import tpu as pltpu
from jax.sharding import PartitionSpec as P

F32 = jnp.float32
BF16 = jnp.bfloat16
MESH = pl.DeviceIdType.MESH

ORDER = [(0, 0), (0, 1), (0, 3), (0, 2), (1, 0), (3, 0), (2, 0), (1, 1),
         (1, 3), (3, 1), (3, 3), (1, 2), (2, 1), (3, 2), (2, 3), (2, 2)]
PLACE = {block: place for place, block in enumerate(ORDER)}
QUARTERS = 4
GROUP_BLOCKS = 4
NT = (((1,), (1,)), ((), ()))
TN = (((0,), (0,)), ((), ()))


def send_lists():
    plus_x = [(0, 0, 0), (0, 0, 1), (0, 0, 2), (0, 1, 0), (0, 0, 3), (0, 1, 2),
              (1, 0, 2), (1, 0, 3), (3, 0, 2), (3, 0, 3), (2, 0, 2), (2, 0, 3),
              (1, 1, 2), (3, 1, 2), (2, 1, 2)]
    flip = (1, 0, 3, 2)
    swap = (2, 3, 0, 1)
    minus_x = [(oy, -ox % 4, flip[q]) for oy, ox, q in plus_x]
    plus_y = [(ox, oy, swap[q]) for oy, ox, q in plus_x]
    minus_y = [(-oy % 4, ox, flip[q]) for oy, ox, q in plus_y]
    return {(0, 1): plus_x, (0, 3): minus_x, (1, 0): plus_y, (3, 0): minus_y}


SENDS = send_lists()
SLOTS = len(SENDS[(0, 1)])


def chain(values, index):
    out = jnp.int32(values[0])
    for k in range(1, len(values)):
        out = jnp.where(index == k, jnp.int32(values[k]), out)
    return out


def expert_kernel(group_size, x_hbm, wg_hbm, wu_hbm, wd_hbm, dout_hbm, route_hbm,
                  dadb_hbm, gu_hbm, dn_hbm, back_hbm, pq_hbm, h_hbm,
                  ag, rt, acc_gu, acc_d, wgu, wd, xb, db, pq, hb, dadb, gs, gg, gsend, grecv,
                  w_sem, own_sem, x_sem, spill_sem, fill_sem, dadb_sem, fin_sem,
                  recv_sem, rrecv_sem, send_sem, rsend_sem,
                  srecv_sem, srrecv_sem, ssend_sem, srsend_sem, gsend_sem, grecv_sem):
    side = math.isqrt(group_size // 2)
    me = lax.axis_index('ep')
    core = lax.rem(me, 2)
    my_x = lax.rem(me // 2, side)
    my_y = me // (2 * side)
    e_local, rows_u, model = xb.shape
    ffn = hb.shape[2]
    cap = x_hbm.shape[2]
    tok = ag.shape[2]
    qrows = tok // QUARTERS
    n_blocks = side * side
    groups = n_blocks // GROUP_BLOCKS
    per_unit = 2 * GROUP_BLOCKS
    tile = 256
    mt_count = model // tile
    ft_count = ffn // tile

    def device(y, x, c):
        return (y * side + x) * 2 + c

    def neighbour(dy, dx):
        return device(lax.rem(my_y + dy, side), lax.rem(my_x + dx, side), core)

    sibling = device(my_y, my_x, 1 - core)

    def origin(p, r):
        oy = chain([b[0] for b in ORDER], p)
        ox = chain([b[1] for b in ORDER], p)
        c = core + r - 2 * core * r
        return device(lax.rem(my_y + side - oy, side), lax.rem(my_x + side - ox, side), c)

    def quarter(r, p, q):
        return ag.at[r, p, pl.ds(q * qrows, qrows)]

    def ici_copy(p_from, p_to, q, to):
        return pltpu.make_async_remote_copy(
            src_ref=quarter(0, p_from, q), dst_ref=quarter(0, p_to, q), send_sem=send_sem,
            recv_sem=recv_sem.at[p_to, q], device_id={'ep': to}, device_id_type=MESH)

    def ici_route(p_from, p_to, to):
        return pltpu.make_async_remote_copy(
            src_ref=rt.at[0, p_from], dst_ref=rt.at[0, p_to], send_sem=rsend_sem,
            recv_sem=rrecv_sem.at[p_to], device_id={'ep': to}, device_id_type=MESH)

    def sib_copy(p, q):
        return pltpu.make_async_remote_copy(
            src_ref=quarter(0, p, q), dst_ref=quarter(1, p, q), send_sem=ssend_sem,
            recv_sem=srecv_sem.at[p, q], device_id={'ep': sibling}, device_id_type=MESH)

    def sib_route(p):
        return pltpu.make_async_remote_copy(
            src_ref=rt.at[0, p], dst_ref=rt.at[1, p], send_sem=srsend_sem,
            recv_sem=srrecv_sem.at[p], device_id={'ep': sibling}, device_id_type=MESH)

    def issue(slot):
        for (dy, dx), sends in SENDS.items():
            oy, ox, q = sends[slot]
            p_from, p_to = PLACE[(oy, ox)], PLACE[((oy + dy) % 4, (ox + dx) % 4)]
            to = neighbour(dy, dx)
            ici_copy(p_from, p_to, q, to).start()
            if q == 0:
                ici_route(p_from, p_to, to).start()

    def service(slot):
        for (dy, dx), sends in SENDS.items():
            oy, ox, q = sends[slot]
            p_to = PLACE[((oy + dy) % 4, (ox + dx) % 4)]
            ici_copy(p_to, p_to, q, me).wait_recv()
            if q == 0:
                ici_route(p_to, p_to, me).wait_recv()
        if slot + 3 < SLOTS:
            issue(slot + 3)
        for (dy, dx), sends in SENDS.items():
            oy, ox, q = sends[slot]
            p_to = PLACE[((oy + dy) % 4, (ox + dx) % 4)]
            sib_copy(p_to, q).start()
            if q == 0:
                sib_route(p_to).start()

    def x_copy(g, e, j):
        src = origin(g * GROUP_BLOCKS + j // 2, j % 2)
        return pltpu.make_async_copy(x_hbm.at[src, e], xb.at[e, pl.ds(j * cap, cap)], x_sem.at[e, j])

    def dadb_copy(g, e, j):
        src = origin(g * GROUP_BLOCKS + j // 2, j % 2)
        return pltpu.make_async_copy(dadb.at[pl.ds(j * cap, cap)], dadb_hbm.at[src, e], dadb_sem.at[j])

    def x_start(g, e):
        for j in range(per_unit):
            x_copy(g, e, j).start()

    def x_wait(g, e):
        for j in range(per_unit):
            x_copy(g, e, j).wait()

    def spill_copies(u, e):
        return (pltpu.make_async_copy(pq.at[e], pq_hbm.at[u], spill_sem.at[e, 0]),
                pltpu.make_async_copy(hb.at[e], h_hbm.at[u], spill_sem.at[e, 1]))

    def fill_copies(u, e):
        return (pltpu.make_async_copy(pq_hbm.at[u], pq.at[e], fill_sem.at[e, 0]),
                pltpu.make_async_copy(h_hbm.at[u], hb.at[e], fill_sem.at[e, 1]))

    w_copies = [pltpu.make_async_copy(wg_hbm, wgu.at[:, :, pl.ds(0, ffn)], w_sem.at[0]),
                pltpu.make_async_copy(wu_hbm, wgu.at[:, :, pl.ds(ffn, ffn)], w_sem.at[1]),
                pltpu.make_async_copy(wd_hbm, wd, w_sem.at[2])]
    own = [pltpu.make_async_copy(dout_hbm, ag.at[0, 0], own_sem.at[0]),
           pltpu.make_async_copy(route_hbm, rt.at[0, 0], own_sem.at[1])]

    for c in own:
        c.start()
    barrier = pltpu.get_barrier_semaphore()

    @pl.loop(1, group_size)
    def _(k):
        pl.semaphore_signal(barrier, inc=1, device_id={'ep': lax.rem(me + k, group_size)}, device_id_type=MESH)

    for c in w_copies[:2]:
        c.start()
    x_start(0, 0)
    x_start(0, 1)
    w_copies[2].start()
    for c in own:
        c.wait()
    pl.semaphore_wait(barrier, group_size - 1)
    for slot in range(3):
        issue(slot)
    for q in range(QUARTERS):
        sib_copy(0, q).start()
    sib_route(0).start()

    @pl.loop(0, mt_count)
    def _(m):
        rows = pl.ds(pl.multiple_of(m * tile, tile), tile)
        for e in range(e_local):
            acc_gu[e, rows] = jnp.zeros((tile, 2 * ffn), F32)

    @pl.loop(0, ft_count)
    def _(m):
        rows = pl.ds(pl.multiple_of(m * tile, tile), tile)
        for e in range(e_local):
            acc_d[e, rows] = jnp.zeros((tile, model), F32)

    for c in w_copies[:2]:
        c.wait()

    @pl.loop(0, groups * e_local)
    def _(u):
        g, e = u // e_local, lax.rem(u, e_local)
        x_wait(g, e)

        @pl.when(u >= e_local)
        def _():
            for c in spill_copies(u - e_local, e):
                c.wait()

        @pl.loop(0, ft_count)
        def _(n):
            lo = pl.ds(pl.multiple_of(n * tile, tile), tile)
            hi = pl.ds(pl.multiple_of(ffn + n * tile, tile), tile)
            x = xb[e]
            a = jnp.dot(x, wgu[e, :, lo], preferred_element_type=F32)
            b = jnp.dot(x, wgu[e, :, hi], preferred_element_type=F32)
            sg = jax.nn.sigmoid(a)
            silu = a * sg
            hb[e, :, lo] = (silu * b).astype(BF16)
            pq[e, :, lo] = b * sg * (1.0 + a * (1.0 - sg))
            pq[e, :, hi] = silu

        for c in spill_copies(u, e):
            c.start()
        nxt = u + e_local
        x_start(lax.rem(nxt // e_local, groups), e)

        for k, at in ((0, 2), (1, 4), (2, 6)):
            @pl.when(u == at)
            def _(k=k):
                service(k)

    for e in range(e_local):
        for c in spill_copies((groups - 1) * e_local + e, e):
            c.wait()
    for e in range(e_local):
        for c in fill_copies(e, e):
            c.start()
    w_copies[2].wait()
    for slot in (3, 4, 5):
        service(slot)

    def hits(r, p, e):
        local = rt[r, p, 0:8] - (me * (e_local * cap) + e * cap).astype(F32)
        hit = (local >= 0.0) & (local < float(cap))
        slot = jnp.max(jnp.where(hit, local, -1.0), axis=0, keepdims=True)
        gate = jnp.sum(jnp.where(hit, rt[r, p, 8:16], 0.0), axis=0, keepdims=True)
        return slot, gate

    @pl.loop(0, groups)
    def _(g):
        def on(step, *slots):
            @pl.when(g == step)
            def _():
                for s in slots:
                    service(s)

        @pl.loop(0, per_unit)
        def _(j):
            p, r = g * GROUP_BLOCKS + j // 2, lax.rem(j, 2)

            @pl.when(r == 1)
            def _():
                for q in range(QUARTERS):
                    sib_copy(p, q).wait_recv()
                sib_route(p).wait_recv()

            rows = pl.ds(pl.multiple_of(j * cap, cap), cap)
            slot_iota = lax.broadcasted_iota(jnp.int32, (cap, tok), 0).astype(F32)
            picks = []
            for e in range(e_local):
                slot, gate = hits(r, p, jnp.int32(e))
                pick = slot_iota == slot
                gs[e, rows] = jnp.broadcast_to(
                    jnp.sum(jnp.where(pick, gate, 0.0), axis=1, keepdims=True), (cap, 128))
                picks.append(jnp.where(pick, 1.0, 0.0).astype(BF16))
            pick = jnp.concatenate(picks, axis=0)
            for n in range(model // 512):
                cols = pl.ds(n * 512, 512)
                d = jnp.dot(pick, ag[r, p, :, cols], preferred_element_type=F32).astype(BF16)
                for e in range(e_local):
                    db[e, rows, cols] = d[e * cap:(e + 1) * cap]

        on(0, 6)
        on(1, 8)

        @pl.loop(0, e_local)
        def _(e):
            x_wait(g, e)
            for c in fill_copies(g * e_local + e, e):
                c.wait()
            gg[...] = jnp.zeros_like(gg)

            @pl.loop(0, mt_count)
            def _(n):
                cols = pl.ds(pl.multiple_of(n * tile, tile), tile)
                y = jnp.dot(hb[e], wd[e, :, cols], preferred_element_type=F32)
                d = db[e, :, cols].astype(F32)
                prod = d * y
                gg[...] += prod[:, :128] + prod[:, 128:]
                gate = gs[e]
                db[e, :, cols] = (d * jnp.concatenate([gate, gate], axis=1)).astype(BF16)

            @pl.when(g * e_local + e > 0)
            def _():
                for j in range(per_unit):
                    dadb_copy(g, e, j).wait()

            @pl.loop(0, ft_count)
            def _(n):
                lo = pl.ds(pl.multiple_of(n * tile, tile), tile)
                hi = pl.ds(pl.multiple_of(ffn + n * tile, tile), tile)
                dh = lax.dot_general(db[e], wd[e, lo, :], NT, preferred_element_type=F32).astype(BF16).astype(F32)
                dadb[:, lo] = (dh * pq[e, :, lo]).astype(BF16)
                dadb[:, hi] = (dh * pq[e, :, hi]).astype(BF16)

            for j in range(per_unit):
                dadb_copy(g, e, j).start()

            gg[...] = jnp.broadcast_to(jnp.sum(gg[...], axis=1, keepdims=True), gg.shape)

            @pl.loop(0, per_unit)
            def _(j):
                p, r = g * GROUP_BLOCKS + j // 2, lax.rem(j, 2)
                rows = pl.ds(pl.multiple_of(j * cap, cap), cap)
                slot, _ = hits(r, p, e)
                pick = lax.broadcasted_iota(jnp.int32, (cap, tok), 0).astype(F32) == slot
                value = jnp.concatenate([gg[rows]] * (tok // 128), axis=1)
                gsend[g * per_unit + j, e] = jnp.sum(jnp.where(pick, value, 0.0), axis=0, keepdims=True)

            @pl.loop(0, mt_count)
            def _(m):
                rows = pl.ds(pl.multiple_of(m * tile, tile), tile)
                for n in range(2):
                    cols = pl.ds(n * ffn, ffn)
                    acc_gu[e, rows, cols] += lax.dot_general(
                        xb[e, :, rows], dadb[:, cols], TN, preferred_element_type=F32)

            @pl.loop(0, ft_count)
            def _(m):
                rows = pl.ds(pl.multiple_of(m * tile, tile), tile)
                for n in range(model // 512):
                    cols = pl.ds(n * 512, 512)
                    acc_d[e, rows, cols] += lax.dot_general(
                        hb[e, :, rows], db[e, :, cols], TN, preferred_element_type=F32)

            @pl.when(g + 1 < groups)
            def _():
                x_start(g + 1, e)
                for c in fill_copies((g + 1) * e_local + e, e):
                    c.start()

            @pl.when(g + 1 == groups)
            def _():
                @pl.loop(0, mt_count)
                def _(m):
                    rows = pl.ds(pl.multiple_of(m * tile, tile), tile)
                    wgu[e, rows] = acc_gu[e, rows].astype(BF16)

                @pl.loop(0, ft_count)
                def _(m):
                    rows = pl.ds(pl.multiple_of(m * tile, tile), tile)
                    wd[e, rows] = acc_d[e, rows].astype(BF16)

                pltpu.make_async_copy(wgu.at[e], gu_hbm.at[e], fin_sem.at[e, 0]).start()
                pltpu.make_async_copy(wd.at[e], dn_hbm.at[e], fin_sem.at[e, 1]).start()

            for at, first, second in ((0, 7, None), (1, 9, 10), (2, 13, 14)):
                slots = (first, second)
                for which in range(2):
                    if slots[which] is not None:
                        @pl.when((g == at) & (e == which))
                        def _(s=slots[which]):
                            service(s)

        on(1, 11, 12)

        @pl.when(g == 0)
        def _():
            grecv[me] = gsend[0]

        @pl.loop(jnp.where(g == 0, 1, 0), per_unit)
        def _(j):
            to = origin(g * GROUP_BLOCKS + j // 2, lax.rem(j, 2))
            pltpu.make_async_remote_copy(
                src_ref=gsend.at[g * per_unit + j], dst_ref=grecv.at[me], send_sem=gsend_sem,
                recv_sem=grecv_sem, device_id={'ep': to}, device_id_type=MESH).start()

    for j in range(per_unit):
        dadb_copy(groups - 1, e_local - 1, j).wait()

    def drain(ref, sem):
        pltpu.make_async_copy(ref, ref, sem).wait()

    drain(ag.at[0, pl.ds(0, n_blocks - 1)], send_sem)
    drain(rt.at[0, pl.ds(0, n_blocks - 1)], rsend_sem)
    drain(ag.at[0], ssend_sem)
    drain(rt.at[0], srsend_sem)
    drain(gsend.at[pl.ds(0, group_size - 1)], gsend_sem)
    drain(grecv.at[pl.ds(0, group_size - 1)], grecv_sem)
    back = pltpu.make_async_copy(grecv, back_hbm, own_sem.at[0])
    back.start()
    back.wait()
    for e in range(e_local):
        pltpu.make_async_copy(wgu.at[e], gu_hbm.at[e], fin_sem.at[e, 0]).wait()
        pltpu.make_async_copy(wd.at[e], dn_hbm.at[e], fin_sem.at[e, 1]).wait()


def run_experts(x_disp, w_gate, w_up, w_down, d_out, route, group_size):
    sources, e_local, cap, model = x_disp.shape
    ffn = w_gate.shape[2]
    tok = d_out.shape[0]
    n_blocks = group_size // 2
    per_unit = 2 * GROUP_BLOCKS
    rows_u = per_unit * cap
    units = n_blocks // GROUP_BLOCKS * e_local
    dma = pltpu.SemaphoreType.DMA
    any_spec = pl.BlockSpec(memory_space=pl.ANY)
    out_shape = [
        jax.ShapeDtypeStruct((sources, e_local, cap, 2 * ffn), BF16),
        jax.ShapeDtypeStruct((e_local, model, 2 * ffn), BF16),
        jax.ShapeDtypeStruct((e_local, ffn, model), BF16),
        jax.ShapeDtypeStruct((group_size, e_local, 1, tok), F32),
        jax.ShapeDtypeStruct((units, rows_u, 2 * ffn), F32),
        jax.ShapeDtypeStruct((units, rows_u, ffn), BF16),
    ]
    scratch = [
        pltpu.VMEM((2, n_blocks, tok, model), BF16),
        pltpu.VMEM((2, n_blocks, 16, tok), F32),
        pltpu.VMEM((e_local, model, 2 * ffn), F32),
        pltpu.VMEM((e_local, ffn, model), F32),
        pltpu.VMEM((e_local, model, 2 * ffn), BF16),
        pltpu.VMEM((e_local, ffn, model), BF16),
        pltpu.VMEM((e_local, rows_u, model), BF16),
        pltpu.VMEM((e_local, rows_u, model), BF16),
        pltpu.VMEM((e_local, rows_u, 2 * ffn), F32),
        pltpu.VMEM((e_local, rows_u, ffn), BF16),
        pltpu.VMEM((rows_u, 2 * ffn), BF16),
        pltpu.VMEM((e_local, rows_u, 128), F32),
        pltpu.VMEM((rows_u, 128), F32),
        pltpu.VMEM((group_size, e_local, 1, tok), F32),
        pltpu.VMEM((group_size, e_local, 1, tok), F32),
        dma((3,)), dma((2,)), dma((e_local, per_unit)), dma((e_local, 2)), dma((e_local, 2)),
        dma((per_unit,)), dma((e_local, 2)),
        dma((n_blocks, QUARTERS)), dma((n_blocks,)), dma, dma,
        dma((n_blocks, QUARTERS)), dma((n_blocks,)), dma, dma, dma, dma,
    ]
    return pl.pallas_call(
        functools.partial(expert_kernel, group_size),
        out_shape=out_shape, in_specs=[any_spec] * 6, out_specs=[any_spec] * 6, scratch_shapes=scratch,
        compiler_params=pltpu.CompilerParams(collective_id=0, has_side_effects=True, vmem_limit_bytes=67043328),
    )(x_disp, w_gate, w_up, w_down, d_out, route)


def finish_kernel(group_size, dadb, wg, wu, gu, dn, back, ids, slots, gx, gg_w, gu_w, gd_w, gate_out):
    sources, _, cap, width = dadb.shape
    ffn = width // 2
    model = gx.shape[3]
    both = dadb[...].reshape(sources * cap, width)
    for n in range(model // 512):
        rows = pl.ds(n * 512, 512)
        out = (lax.dot_general(both[:, :ffn], wg[0, rows], NT, preferred_element_type=F32)
               + lax.dot_general(both[:, ffn:], wu[0, rows], NT, preferred_element_type=F32))
        gx[:, 0, :, rows] = out.astype(BF16).reshape(sources, cap, 512)
    gg_w[...] = gu[:, :, :ffn]
    gu_w[...] = gu[:, :, ffn:]
    gd_w[...] = dn[...]

    @pl.when((pl.program_id(0) == 0) & (pl.program_id(1) == 0))
    def _():
        e_local = back.shape[1]
        total = jnp.zeros(gate_out.shape, F32)
        for d in range(group_size):
            for e in range(e_local):
                total += jnp.where(ids[...] == d * e_local + e, back[d, e], 0.0)
        gate_out[...] = jnp.where(slots[...] >= 0, total, 0.0)


def run_finish(dadb, w_gate, w_up, gu, dn, back, ids, slots, group_size):
    sources, e_local, cap, width = dadb.shape
    model, ffn = w_gate.shape[1:]
    steps = 4
    s_blk, m_blk, f_blk = sources // steps, model // steps, ffn // steps
    tok = ids.shape[1]
    whole = lambda shape: pl.BlockSpec(shape, lambda e, i: (0,) * len(shape))
    return pl.pallas_call(
        functools.partial(finish_kernel, group_size),
        grid=(e_local, steps),
        in_specs=[
            pl.BlockSpec((s_blk, 1, cap, width), lambda e, i: (i, e, 0, 0)),
            pl.BlockSpec((1, model, ffn), lambda e, i: (e, 0, 0)),
            pl.BlockSpec((1, model, ffn), lambda e, i: (e, 0, 0)),
            pl.BlockSpec((1, m_blk, width), lambda e, i: (e, i, 0)),
            pl.BlockSpec((1, f_blk, model), lambda e, i: (e, i, 0)),
            whole(back.shape), whole((8, tok)), whole((8, tok)),
        ],
        out_specs=[
            pl.BlockSpec((s_blk, 1, cap, model), lambda e, i: (i, e, 0, 0)),
            pl.BlockSpec((1, m_blk, ffn), lambda e, i: (e, i, 0)),
            pl.BlockSpec((1, m_blk, ffn), lambda e, i: (e, i, 0)),
            pl.BlockSpec((1, f_blk, model), lambda e, i: (e, i, 0)),
            whole((8, tok)),
        ],
        out_shape=[
            jax.ShapeDtypeStruct((sources, e_local, cap, model), BF16),
            jax.ShapeDtypeStruct((e_local, model, ffn), BF16),
            jax.ShapeDtypeStruct((e_local, model, ffn), BF16),
            jax.ShapeDtypeStruct((e_local, ffn, model), BF16),
            jax.ShapeDtypeStruct((8, tok), F32),
        ],
    )(dadb, w_gate, w_up, gu, dn, back, ids, slots)


def solution(mesh):
    group_size = mesh.shape['ep']

    def local_step(x_disp, w_gate, w_up, w_down, d_out, slot_idx, expert_id, gate_wt):
        cap = x_disp.shape[2]
        top_k = slot_idx.shape[1]
        pad = ((0, 8 - top_k), (0, 0))
        slots = jnp.pad(slot_idx.T, pad, constant_values=-1)
        ids = jnp.pad(expert_id.T, pad)
        pos = jnp.where(slots >= 0, ids * cap + slots, -1).astype(F32)
        route = jnp.concatenate([pos, jnp.pad(gate_wt.T, pad)], axis=0)
        dadb, gu, dn, back, _, _ = run_experts(x_disp, w_gate, w_up, w_down, d_out, route, group_size)
        grad_x, grad_w_gate, grad_w_up, grad_w_down, gate = run_finish(
            dadb, w_gate, w_up, gu, dn, back, ids, slots, group_size)
        return grad_x, grad_w_gate, grad_w_up, grad_w_down, gate[:top_k].T

    token_place = P(('dp', 'ep'), None)
    weight_place = P('ep', None, None)
    slot_place = P('dp', 'ep', None, None)
    grad_place = P(('dp', 'ep'), None, None)
    return jax.shard_map(local_step, mesh=mesh,
                         in_specs=(slot_place, weight_place, weight_place, weight_place, token_place, token_place, token_place, token_place),
                         out_specs=(slot_place, grad_place, grad_place, grad_place, token_place),
                         check_vma=False)
```

time: 320 us -> 143 us (0.45)
  Pallas kernels: 0 us -> 138 us
  waiting for transfers between devices: 106 us -> 0 us
  matrix products: 99.5 us -> 0 us
  local copies, waits for them, and re-layouts: 73.4 us -> 1.29 us
  starting transfers between devices: 29.3 us -> 0 us
  other arithmetic: 10.3 us -> 2.63 us
    pallas_call x0 -> x2, Pallas kernels: none -> 138 us  [the longest x1 118 us: run_experts(): pl.pallas_call(functools.partial(expert_kernel, group_size), out_shape=ou...]
    all_to_all x3 -> x0, waiting for transfers between devices: 106 us -> none  [the longest x1 106 us: local_step(): out_rows = lax.all_to_all(send_rows, 'ep', 0, 0, tiled=True)]
    dot_general x9 -> x0, matrix products: 99.5 us -> none  [the longest x1 15.1 us: expert_backward(): jnp.einsum('secf,edf->secd', grad_pre_up, w_up, preferred_element_type=jn...]
    gather x5 -> x0, local copies, waits for them, and re-layouts: 46.5 us -> none  [the longest x1 20.5 us: local_step(): jnp.take(d_out, owner_ids // top_k, axis=0, mode='fill', fill_value=0)]
    all_to_all x3 -> x0, starting transfers between devices: 29.3 us -> none  [the longest x1 13.8 us: local_step(): back_rows = lax.all_to_all(gate_grad_rows, 'ep', 0, 0, tiled=True)]
    unnamed x18 -> x0, local copies, waits for them, and re-layouts: 18.5 us -> none
    select_n x5 -> x0, other arithmetic: 9.69 us -> none  [the longest x1 8.17 us: local_step(): jnp.take(d_out, owner_ids // top_k, axis=0, mode='fill', fill_value=0)]
    scatter x1 -> x0, local copies, waits for them, and re-layouts: 6.19 us -> none  [local_step(): jnp.full((slot_count,), tok_dev * top_k, jnp.int32).at[flat_pos.reshape(-1)]]
  transfers between devices with their start and end apart: 3 -> 0, of which waited for: 1 -> 0; matrix products, arithmetic and copies ran while one was open for 26% -> 0% of each run, Pallas kernels for 0% -> 0%
where the time goes in v1:
time: 143 us
  Pallas kernels  138 us (97%)
  other arithmetic  2.63 us (2%)
    pallas_call x1, Pallas kernels, run_experts(): pl.pallas_call(functools.partial(expert_kernel, group_size), out_shape=ou...  118 us
    pallas_call x1, Pallas kernels, run_finish(): pl.pallas_call(functools.partial(finish_kernel, group_size), grid=(e_loca...  20.4 us

profile of v1, /device:TPU:97, one launch (start us, length us, event | category | flops | bytes accessed | tf_op | source)
XLA Modules:
  0.0 142.9 jit_solution(11584692753969311952)
XLA Ops:
  0.6 1.3 fusion
  2.0 1.3 select_maximum_fusion.route_hbm
  3.3 117.9 %shard_map.119 = (bf16[32,2,48,1024]{3,2,1,0:T(8,128)(2,1)}, bf16[2,1536,1024]{2,1,0:T(8,128)(2,1)}, bf16[2,512,1536]{2,1,0:T(8,128)(2,1)}, f32[32,2,1,256]{3,2,...) custom-call(bf16[32,2,48,1536]{3,2,1,0:T(8,128)(2,1)} %x_hbm.1, bf16[2,1536,512]{2,1,0:T(8,128)(2,1)} %wg.1, ...), custom_call_target="tpu_custom_call" | custom-call | tf_op jit(solution)/shard_map/pallas_call | solution.py:447
  121.2 20.4 %shard_map.120 = (bf16[32,2,48,1536]{3,2,1,0:T(8,128)(2,1)}, bf16[2,1536,512]{2,1,0:T(8,128)(2,1)}, bf16[2,1536,512]{2,1,0:T(8,128)(2,1)}, bf16[2,512,1536]{2,1,0:T(8,128)(2,1)}, f32[8,256]{1,0:T(8,128)}) custom-call(bf16[32,2,48,1024]{3,2,1,0:T(8,128)(2,1)} %get-tuple-element.14.dadb, bf16[2,1536,512]{2,1,0:T(8,128)(2,1)} %wg.1, bf16[2,1536,512]{2,1,0:T(8,128)(2,1)} %wu.1, ...), custom_call_target="tpu_custom_call" | custom-call | tf_op jit(solution)/shard_map/pallas_call | solution.py:485
  141.6 1.3 slice_bitcast_fusion

commit v2 on v1

--- a/solution.py
+++ b/solution.py
@@ -12,23 +12,37 @@
 BF16 = jnp.bfloat16
 MESH = pl.DeviceIdType.MESH
 
-ORDER = [(0, 0), (0, 1), (0, 3), (0, 2), (1, 0), (3, 0), (2, 0), (1, 1),
-         (1, 3), (3, 1), (3, 3), (1, 2), (2, 1), (3, 2), (2, 3), (2, 2)]
+ORDER = [(0, 0), (0, 1), (0, 3), (1, 0), (3, 0), (0, 2), (2, 0), (1, 1),
+         (1, 2), (3, 1), (1, 3), (3, 3), (3, 2), (2, 1), (2, 3), (2, 2)]
 PLACE = {block: place for place, block in enumerate(ORDER)}
+
+
+def packed(values):
+    total = sum(v << (2 * k) for k, v in enumerate(values))
+    return total - 2 ** 32 if total >= 2 ** 31 else total
+
+
+ORIGIN_Y, ORIGIN_X = packed([b[0] for b in ORDER]), packed([b[1] for b in ORDER])
 QUARTERS = 4
-GROUP_BLOCKS = 4
+UNIT_BLOCKS = 4
+STEP_BLOCKS = 2
+BEFORE = {0: (3,), 3: (7,), 4: (9, 10), 6: (13,)}
+BETWEEN = {0: (4,), 1: (5,), 2: (6,), 3: (8,), 4: (11,), 5: (12,)}
+AFTER = {6: (14,)}
 NT = (((1,), (1,)), ((), ()))
 TN = (((0,), (0,)), ((), ()))
 
 
 def send_lists():
-    plus_x = [(0, 0, 0), (0, 0, 1), (0, 0, 2), (0, 1, 0), (0, 0, 3), (0, 1, 2),
-              (1, 0, 2), (1, 0, 3), (3, 0, 2), (3, 0, 3), (2, 0, 2), (2, 0, 3),
-              (1, 1, 2), (3, 1, 2), (2, 1, 2)]
+    own = [(0, 0, 0), (0, 0, 1), (0, 0, 2), (0, 0, 3), (0, 1, 0), (0, 1, 2)]
+    plus_x = own + [(1, 0, 2), (1, 0, 3), (3, 0, 2), (1, 1, 2), (3, 0, 3), (2, 0, 2),
+                    (3, 1, 2), (2, 0, 3), (2, 1, 2)]
+    swap = (2, 3, 0, 1)
     flip = (1, 0, 3, 2)
-    swap = (2, 3, 0, 1)
+    plus_y = [(ox, oy, swap[q]) for oy, ox, q in own]
+    plus_y += [(0, 1, 0), (0, 1, 1), (0, 2, 0), (0, 2, 1), (0, 3, 0), (0, 3, 1),
+               (1, 1, 0), (1, 3, 0), (1, 2, 0)]
     minus_x = [(oy, -ox % 4, flip[q]) for oy, ox, q in plus_x]
-    plus_y = [(ox, oy, swap[q]) for oy, ox, q in plus_x]
     minus_y = [(-oy % 4, ox, flip[q]) for oy, ox, q in plus_y]
     return {(0, 1): plus_x, (0, 3): minus_x, (1, 0): plus_y, (3, 0): minus_y}
 
@@ -37,16 +51,9 @@
 SLOTS = len(SENDS[(0, 1)])
 
 
-def chain(values, index):
-    out = jnp.int32(values[0])
-    for k in range(1, len(values)):
-        out = jnp.where(index == k, jnp.int32(values[k]), out)
-    return out
-
-
 def expert_kernel(group_size, x_hbm, wg_hbm, wu_hbm, wd_hbm, dout_hbm, route_hbm,
                   dadb_hbm, gu_hbm, dn_hbm, back_hbm, pq_hbm, h_hbm,
-                  ag, rt, acc_gu, acc_d, wgu, wd, xb, db, pq, hb, dadb, gs, gg, gsend, grecv,
+                  ag, rt, acc_gu, acc_d, wgu, wd, xb, db, pq, hb, dadb, gg, gsend, grecv,
                   w_sem, own_sem, x_sem, spill_sem, fill_sem, dadb_sem, fin_sem,
                   recv_sem, rrecv_sem, send_sem, rsend_sem,
                   srecv_sem, srrecv_sem, ssend_sem, srsend_sem, gsend_sem, grecv_sem):
@@ -56,13 +63,16 @@
     my_x = lax.rem(me // 2, side)
     my_y = me // (2 * side)
     e_local, rows_u, model = xb.shape
+    rows_s = dadb.shape[1]
     ffn = hb.shape[2]
     cap = x_hbm.shape[2]
     tok = ag.shape[2]
     qrows = tok // QUARTERS
     n_blocks = side * side
-    groups = n_blocks // GROUP_BLOCKS
-    per_unit = 2 * GROUP_BLOCKS
+    units = n_blocks // UNIT_BLOCKS
+    steps = n_blocks // STEP_BLOCKS
+    per_unit = 2 * UNIT_BLOCKS
+    per_step = 2 * STEP_BLOCKS
     tile = 256
     mt_count = model // tile
     ft_count = ffn // tile
@@ -76,8 +86,8 @@
     sibling = device(my_y, my_x, 1 - core)
 
     def origin(p, r):
-        oy = chain([b[0] for b in ORDER], p)
-        ox = chain([b[1] for b in ORDER], p)
+        oy = lax.shift_right_logical(jnp.int32(ORIGIN_Y), 2 * p) & 3
+        ox = lax.shift_right_logical(jnp.int32(ORIGIN_X), 2 * p) & 3
         c = core + r - 2 * core * r
         return device(lax.rem(my_y + side - oy, side), lax.rem(my_x + side - ox, side), c)
 
@@ -129,29 +139,31 @@
             if q == 0:
                 sib_route(p_to).start()
 
-    def x_copy(g, e, j):
-        src = origin(g * GROUP_BLOCKS + j // 2, j % 2)
-        return pltpu.make_async_copy(x_hbm.at[src, e], xb.at[e, pl.ds(j * cap, cap)], x_sem.at[e, j])
-
-    def dadb_copy(g, e, j):
-        src = origin(g * GROUP_BLOCKS + j // 2, j % 2)
-        return pltpu.make_async_copy(dadb.at[pl.ds(j * cap, cap)], dadb_hbm.at[src, e], dadb_sem.at[j])
-
-    def x_start(g, e):
-        for j in range(per_unit):
-            x_copy(g, e, j).start()
-
-    def x_wait(g, e):
-        for j in range(per_unit):
-            x_copy(g, e, j).wait()
+    def x_copy(block, j, e, row, sem):
+        src = origin(block + j // 2, j % 2)
+        return pltpu.make_async_copy(x_hbm.at[src, e], xb.at[e, pl.ds(row + j * cap, cap)], x_sem.at[e, sem + j])
+
+    def unit_x(g, e):
+        return [x_copy(g * UNIT_BLOCKS, j, e, 0, 0) for j in range(per_unit)]
+
+    def half_rows(t):
+        return pl.multiple_of(lax.rem(t, 2) * rows_s, rows_s)
+
+    def step_fill(t, e):
+        row = half_rows(t)
+        here, u = pl.ds(row, rows_s), (t // 2) * e_local + e
+        half = lax.rem(t, 2)
+        return ([x_copy(t * STEP_BLOCKS, j, e, row, half * per_step) for j in range(per_step)]
+                + [pltpu.make_async_copy(pq_hbm.at[u, here], pq.at[e, here], fill_sem.at[e, half, 0]),
+                   pltpu.make_async_copy(h_hbm.at[u, here], hb.at[e, here], fill_sem.at[e, half, 1])])
+
+    def dadb_copy(t, e, j):
+        src = origin(t * STEP_BLOCKS + j // 2, j % 2)
+        return pltpu.make_async_copy(dadb.at[e, pl.ds(j * cap, cap)], dadb_hbm.at[src, e], dadb_sem.at[e, j])
 
     def spill_copies(u, e):
         return (pltpu.make_async_copy(pq.at[e], pq_hbm.at[u], spill_sem.at[e, 0]),
                 pltpu.make_async_copy(hb.at[e], h_hbm.at[u], spill_sem.at[e, 1]))
-
-    def fill_copies(u, e):
-        return (pltpu.make_async_copy(pq_hbm.at[u], pq.at[e], fill_sem.at[e, 0]),
-                pltpu.make_async_copy(h_hbm.at[u], hb.at[e], fill_sem.at[e, 1]))
 
     w_copies = [pltpu.make_async_copy(wg_hbm, wgu.at[:, :, pl.ds(0, ffn)], w_sem.at[0]),
                 pltpu.make_async_copy(wu_hbm, wgu.at[:, :, pl.ds(ffn, ffn)], w_sem.at[1]),
@@ -169,8 +181,9 @@
 
     for c in w_copies[:2]:
         c.start()
-    x_start(0, 0)
-    x_start(0, 1)
+    for e in range(e_local):
+        for c in unit_x(0, e):
+            c.start()
     w_copies[2].start()
     for c in own:
         c.wait()
@@ -196,10 +209,11 @@
     for c in w_copies[:2]:
         c.wait()
 
-    @pl.loop(0, groups * e_local)
+    @pl.loop(0, units * e_local)
     def _(u):
         g, e = u // e_local, lax.rem(u, e_local)
-        x_wait(g, e)
+        for c in unit_x(g, e):
+            c.wait()
 
         @pl.when(u >= e_local)
         def _():
@@ -221,8 +235,11 @@
 
         for c in spill_copies(u, e):
             c.start()
-        nxt = u + e_local
-        x_start(lax.rem(nxt // e_local, groups), e)
+
+        @pl.when(g + 1 < units)
+        def _():
+            for c in unit_x(g + 1, e):
+                c.start()
 
         for k, at in ((0, 2), (1, 4), (2, 6)):
             @pl.when(u == at)
@@ -230,14 +247,13 @@
                 service(k)
 
     for e in range(e_local):
-        for c in spill_copies((groups - 1) * e_local + e, e):
+        for c in spill_copies((units - 1) * e_local + e, e):
             c.wait()
-    for e in range(e_local):
-        for c in fill_copies(e, e):
-            c.start()
+    for t in range(2):
+        for e in range(e_local):
+            for c in step_fill(jnp.int32(t), e):
+                c.start()
     w_copies[2].wait()
-    for slot in (3, 4, 5):
-        service(slot)
 
     def hits(r, p, e):
         local = rt[r, p, 0:8] - (me * (e_local * cap) + e * cap).astype(F32)
@@ -246,110 +262,96 @@
         gate = jnp.sum(jnp.where(hit, rt[r, p, 8:16], 0.0), axis=0, keepdims=True)
         return slot, gate
 
-    @pl.loop(0, groups)
-    def _(g):
-        def on(step, *slots):
-            @pl.when(g == step)
-            def _():
-                for s in slots:
-                    service(s)
-
-        @pl.loop(0, per_unit)
-        def _(j):
-            p, r = g * GROUP_BLOCKS + j // 2, lax.rem(j, 2)
-
-            @pl.when(r == 1)
-            def _():
-                for q in range(QUARTERS):
-                    sib_copy(p, q).wait_recv()
-                sib_route(p).wait_recv()
-
-            rows = pl.ds(pl.multiple_of(j * cap, cap), cap)
-            slot_iota = lax.broadcasted_iota(jnp.int32, (cap, tok), 0).astype(F32)
-            picks = []
-            for e in range(e_local):
-                slot, gate = hits(r, p, jnp.int32(e))
-                pick = slot_iota == slot
-                gs[e, rows] = jnp.broadcast_to(
-                    jnp.sum(jnp.where(pick, gate, 0.0), axis=1, keepdims=True), (cap, 128))
-                picks.append(jnp.where(pick, 1.0, 0.0).astype(BF16))
-            pick = jnp.concatenate(picks, axis=0)
-            for n in range(model // 512):
-                cols = pl.ds(n * 512, 512)
-                d = jnp.dot(pick, ag[r, p, :, cols], preferred_element_type=F32).astype(BF16)
+    def on(table, t):
+        for step, slots in table.items():
+            @pl.when(t == step)
+            def _(slots=slots):
+                for k in slots:
+                    service(k)
+
+    slot_iota = lax.broadcasted_iota(jnp.int32, (cap, tok), 0).astype(F32)
+
+    @pl.loop(0, steps)
+    def _(t):
+        on(BEFORE, t)
+        half = half_rows(t)
+        here = pl.ds(half, rows_s)
+
+        @pl.loop(0, STEP_BLOCKS)
+        def _(i):
+            p = t * STEP_BLOCKS + i
+            for q in range(QUARTERS):
+                sib_copy(p, q).wait_recv()
+            sib_route(p).wait_recv()
+            for r in range(2):
+                picks, gates = [], []
                 for e in range(e_local):
-                    db[e, rows, cols] = d[e * cap:(e + 1) * cap]
-
-        on(0, 6)
-        on(1, 8)
+                    slot, gate = hits(r, p, e)
+                    pick = slot_iota == slot
+                    gates.append(jnp.sum(jnp.where(pick, gate, 0.0), axis=1, keepdims=True))
+                    picks.append(jnp.where(pick, 1.0, 0.0).astype(BF16))
+                pick = jnp.concatenate(picks, axis=0)
+                row = pl.multiple_of((2 * i + r) * cap, cap)
+                for n in range(model // 512):
+                    cols = pl.ds(n * 512, 512)
+                    d = jnp.dot(pick, ag[r, p, :, cols], preferred_element_type=F32)
+                    for e in range(e_local):
+                        d_e = d[e * cap:(e + 1) * cap]
+                        db[e, pl.ds(row, cap), cols] = d_e.astype(BF16)
+                        db[e, pl.ds(rows_s + row, cap), cols] = (d_e * gates[e]).astype(BF16)
 
         @pl.loop(0, e_local)
         def _(e):
-            x_wait(g, e)
-            for c in fill_copies(g * e_local + e, e):
+            for c in step_fill(t, e):
                 c.wait()
+
+            @pl.when(t > 0)
+            def _():
+                for j in range(per_step):
+                    dadb_copy(t, e, j).wait()
+
             gg[...] = jnp.zeros_like(gg)
-
-            @pl.loop(0, mt_count)
-            def _(n):
-                cols = pl.ds(pl.multiple_of(n * tile, tile), tile)
-                y = jnp.dot(hb[e], wd[e, :, cols], preferred_element_type=F32)
-                d = db[e, :, cols].astype(F32)
-                prod = d * y
-                gg[...] += prod[:, :128] + prod[:, 128:]
-                gate = gs[e]
-                db[e, :, cols] = (d * jnp.concatenate([gate, gate], axis=1)).astype(BF16)
-
-            @pl.when(g * e_local + e > 0)
-            def _():
-                for j in range(per_unit):
-                    dadb_copy(g, e, j).wait()
 
             @pl.loop(0, ft_count)
             def _(n):
                 lo = pl.ds(pl.multiple_of(n * tile, tile), tile)
                 hi = pl.ds(pl.multiple_of(ffn + n * tile, tile), tile)
-                dh = lax.dot_general(db[e], wd[e, lo, :], NT, preferred_element_type=F32).astype(BF16).astype(F32)
-                dadb[:, lo] = (dh * pq[e, :, lo]).astype(BF16)
-                dadb[:, hi] = (dh * pq[e, :, hi]).astype(BF16)
-
-            for j in range(per_unit):
-                dadb_copy(g, e, j).start()
-
-            gg[...] = jnp.broadcast_to(jnp.sum(gg[...], axis=1, keepdims=True), gg.shape)
-
-            @pl.loop(0, per_unit)
-            def _(j):
-                p, r = g * GROUP_BLOCKS + j // 2, lax.rem(j, 2)
-                rows = pl.ds(pl.multiple_of(j * cap, cap), cap)
-                slot, _ = hits(r, p, e)
-                pick = lax.broadcasted_iota(jnp.int32, (cap, tok), 0).astype(F32) == slot
-                value = jnp.concatenate([gg[rows]] * (tok // 128), axis=1)
-                gsend[g * per_unit + j, e] = jnp.sum(jnp.where(pick, value, 0.0), axis=0, keepdims=True)
-
-            @pl.loop(0, mt_count)
+                both = lax.dot_general(db[e], wd[e, lo, :], NT, preferred_element_type=F32)
+                prod = hb[e, here, lo].astype(F32) * both[:rows_s]
+                gg[...] += prod[:, :128] + prod[:, 128:]
+                dh = both[rows_s:].astype(BF16).astype(F32)
+                dadb[e, :, lo] = (dh * pq[e, here, lo]).astype(BF16)
+                dadb[e, :, hi] = (dh * pq[e, here, hi]).astype(BF16)
+
+            for j in range(per_step):
+                dadb_copy(t, e, j).start()
+
+            total = jnp.broadcast_to(jnp.sum(gg[...], axis=1, keepdims=True), gg.shape)
+            for j in range(per_step):
+                slot, _ = hits(j % 2, t * STEP_BLOCKS + j // 2, e)
+                value = jnp.concatenate([total[j * cap:(j + 1) * cap]] * (tok // 128), axis=1)
+                gsend[t * per_step + j, e] = jnp.sum(
+                    jnp.where(slot_iota == slot, value, 0.0), axis=0, keepdims=True)
+
+            @pl.loop(0, model // 512)
             def _(m):
-                rows = pl.ds(pl.multiple_of(m * tile, tile), tile)
+                rows = pl.ds(pl.multiple_of(m * 512, 512), 512)
                 for n in range(2):
                     cols = pl.ds(n * ffn, ffn)
                     acc_gu[e, rows, cols] += lax.dot_general(
-                        xb[e, :, rows], dadb[:, cols], TN, preferred_element_type=F32)
-
-            @pl.loop(0, ft_count)
-            def _(m):
-                rows = pl.ds(pl.multiple_of(m * tile, tile), tile)
-                for n in range(model // 512):
-                    cols = pl.ds(n * 512, 512)
-                    acc_d[e, rows, cols] += lax.dot_general(
-                        hb[e, :, rows], db[e, :, cols], TN, preferred_element_type=F32)
-
-            @pl.when(g + 1 < groups)
+                        xb[e, here, rows], dadb[e, :, cols], TN, preferred_element_type=F32)
+
+            for n in range(model // 512):
+                cols = pl.ds(n * 512, 512)
+                acc_d[e, :, cols] += lax.dot_general(
+                    hb[e, here, :], db[e, rows_s:, cols], TN, preferred_element_type=F32)
+
+            @pl.when(t + 2 < steps)
             def _():
-                x_start(g + 1, e)
-                for c in fill_copies((g + 1) * e_local + e, e):
+                for c in step_fill(t + 2, e):
                     c.start()
 
-            @pl.when(g + 1 == groups)
+            @pl.when(t + 1 == steps)
             def _():
                 @pl.loop(0, mt_count)
                 def _(m):
@@ -364,29 +366,28 @@
                 pltpu.make_async_copy(wgu.at[e], gu_hbm.at[e], fin_sem.at[e, 0]).start()
                 pltpu.make_async_copy(wd.at[e], dn_hbm.at[e], fin_sem.at[e, 1]).start()
 
-            for at, first, second in ((0, 7, None), (1, 9, 10), (2, 13, 14)):
-                slots = (first, second)
-                for which in range(2):
-                    if slots[which] is not None:
-                        @pl.when((g == at) & (e == which))
-                        def _(s=slots[which]):
-                            service(s)
-
-        on(1, 11, 12)
-
-        @pl.when(g == 0)
+            for step, slots in BETWEEN.items():
+                @pl.when((t == step) & (e == 0))
+                def _(slots=slots):
+                    for k in slots:
+                        service(k)
+
+        on(AFTER, t)
+
+        @pl.when(t == 0)
         def _():
             grecv[me] = gsend[0]
 
-        @pl.loop(jnp.where(g == 0, 1, 0), per_unit)
+        @pl.loop(jnp.where(t == 0, 1, 0), per_step)
         def _(j):
-            to = origin(g * GROUP_BLOCKS + j // 2, lax.rem(j, 2))
+            to = origin(t * STEP_BLOCKS + j // 2, lax.rem(j, 2))
             pltpu.make_async_remote_copy(
-                src_ref=gsend.at[g * per_unit + j], dst_ref=grecv.at[me], send_sem=gsend_sem,
+                src_ref=gsend.at[t * per_step + j], dst_ref=grecv.at[me], send_sem=gsend_sem,
                 recv_sem=grecv_sem, device_id={'ep': to}, device_id_type=MESH).start()
 
-    for j in range(per_unit):
-        dadb_copy(groups - 1, e_local - 1, j).wait()
+    for e in range(e_local):
+        for j in range(per_step):
+            dadb_copy(jnp.int32(steps - 1), e, j).wait()
 
     def drain(ref, sem):
         pltpu.make_async_copy(ref, ref, sem).wait()
@@ -410,9 +411,11 @@
     ffn = w_gate.shape[2]
     tok = d_out.shape[0]
     n_blocks = group_size // 2
-    per_unit = 2 * GROUP_BLOCKS
+    per_unit = 2 * UNIT_BLOCKS
     rows_u = per_unit * cap
-    units = n_blocks // GROUP_BLOCKS * e_local
+    per_step = 2 * STEP_BLOCKS
+    rows_s = per_step * cap
+    units = n_blocks // UNIT_BLOCKS * e_local
     dma = pltpu.SemaphoreType.DMA
     any_spec = pl.BlockSpec(memory_space=pl.ANY)
     out_shape = [
@@ -431,16 +434,15 @@
         pltpu.VMEM((e_local, model, 2 * ffn), BF16),
         pltpu.VMEM((e_local, ffn, model), BF16),
         pltpu.VMEM((e_local, rows_u, model), BF16),
-        pltpu.VMEM((e_local, rows_u, model), BF16),
+        pltpu.VMEM((e_local, 2 * rows_s, model), BF16),
         pltpu.VMEM((e_local, rows_u, 2 * ffn), F32),
         pltpu.VMEM((e_local, rows_u, ffn), BF16),
-        pltpu.VMEM((rows_u, 2 * ffn), BF16),
-        pltpu.VMEM((e_local, rows_u, 128), F32),
-        pltpu.VMEM((rows_u, 128), F32),
+        pltpu.VMEM((e_local, rows_s, 2 * ffn), BF16),
+        pltpu.VMEM((rows_s, 128), F32),
         pltpu.VMEM((group_size, e_local, 1, tok), F32),
         pltpu.VMEM((group_size, e_local, 1, tok), F32),
-        dma((3,)), dma((2,)), dma((e_local, per_unit)), dma((e_local, 2)), dma((e_local, 2)),
-        dma((per_unit,)), dma((e_local, 2)),
+        dma((3,)), dma((2,)), dma((e_local, per_unit)), dma((e_local, 2)), dma((e_local, 2, 2)),
+        dma((e_local, per_step)), dma((e_local, 2)),
         dma((n_blocks, QUARTERS)), dma((n_blocks,)), dma, dma,
         dma((n_blocks, QUARTERS)), dma((n_blocks,)), dma, dma, dma, dma,
     ]

time: 143 us -> 130 us (0.909)
  Pallas kernels: 138 us -> 124 us
    pallas_call x1, Pallas kernels: 118 us -> 104 us  [run_experts(): pl.pallas_call(functools.partial(expert_kernel, group_size), out_shape=ou...]
where the time goes in v2:
time: 130 us; the launch traced here: 129 us
  Pallas kernels  124 us (95%)
  other arithmetic  2.63 us (2%)
    pallas_call x1, Pallas kernels, run_experts(): pl.pallas_call(functools.partial(expert_kernel, group_size), out_shape=ou...  104 us
    pallas_call x1, Pallas kernels, run_finish(): pl.pallas_call(functools.partial(finish_kernel, group_size), grid=(e_loca...  20.4 us

profile of v2, /device:TPU:97, one launch (start us, length us, event | category | flops | bytes accessed | tf_op | source)
XLA Modules:
  0.0 129.0 jit_solution(1293382895269993303)
XLA Ops:
  0.6 1.3 %fusion = (s32[8,256]{1,0:T(8,128)}, f32[8,256]{1,0:T(8,128)S(1)}, s32[8,256]{1,0:T(8,128)}) fusion(s32[6,256]{1,0:T(8,128)} %bitcast.5, s32[6,256]{1,0:T(8,128)} %bitcast.6), kind=kLoop, calls=%fused_computation.4 | loop fusion | flops 10240 | bytes 36864 | tf_op jit(solution)/shard_map/jit(_pad)/pad | solution.py:522
  2.0 1.3 %select_maximum_fusion.route_hbm = f32[16,256]{1,0:T(8,128)} fusion(f32[6,256]{1,0:T(8,128)} %bitcast.7, f32[8,256]{1,0:T(8,128)S(1)} %get-tuple-element.24), kind=kLoop, calls=%fused_computation | loop fusion | flops 12288 | bytes 30720 | tf_op jit(solution)/shard_map/concatenate | solution.py:525
  3.3 104.0 %shard_map.119 = (bf16[32,2,48,1024]{3,2,1,0:T(8,128)(2,1)}, bf16[2,1536,1024]{2,1,0:T(8,128)(2,1)}, bf16[2,512,1536]{2,1,0:T(8,128)(2,1)}, f32[32,2,1,256]{3,2,...) custom-call(bf16[32,2,48,1536]{3,2,1,0:T(8,128)(2,1)} %x_hbm.1, bf16[2,1536,512]{2,1,0:T(8,128)(2,1)} %wg.1, ...), custom_call_target="tpu_custom_call" | custom-call | tf_op jit(solution)/shard_map/pallas_call | solution.py:449
  107.3 20.4 %shard_map.120 = (bf16[32,2,48,1536]{3,2,1,0:T(8,128)(2,1)}, bf16[2,1536,512]{2,1,0:T(8,128)(2,1)}, bf16[2,1536,512]{2,1,0:T(8,128)(2,1)}, bf16[2,512,1536]{2,1,0:T(8,128)(2,1)}, f32[8,256]{1,0:T(8,128)}) custom-call(bf16[32,2,48,1024]{3,2,1,0:T(8,128)(2,1)} %get-tuple-element.14.dadb, bf16[2,1536,512]{2,1,0:T(8,128)(2,1)} %wg.1, bf16[2,1536,512]{2,1,0:T(8,128)(2,1)} %wu.1, ...), custom_call_target="tpu_custom_call" | custom-call | tf_op jit(solution)/shard_map/pallas_call | solution.py:487
  127.7 1.3 %slice_bitcast_fusion = f32[256,6]{0,1:T(8,128)} fusion(f32[8,256]{1,0:T(8,128)} %get-tuple-element.22), kind=kLoop, calls=%fused_computation.2 | loop fusion | bytes 12288 | tf_op jit(solution)/shard_map/transpose | solution.py:529

commit v3 on v2

--- a/solution.py
+++ b/solution.py
@@ -53,7 +53,7 @@
 
 def expert_kernel(group_size, x_hbm, wg_hbm, wu_hbm, wd_hbm, dout_hbm, route_hbm,
                   dadb_hbm, gu_hbm, dn_hbm, back_hbm, pq_hbm, h_hbm,
-                  ag, rt, acc_gu, acc_d, wgu, wd, xb, db, pq, hb, dadb, gg, gsend, grecv,
+                  ag, rt, acc_gu, acc_d, wgu, wd, xb, db, pq, hb, gsend, grecv,
                   w_sem, own_sem, x_sem, spill_sem, fill_sem, dadb_sem, fin_sem,
                   recv_sem, rrecv_sem, send_sem, rsend_sem,
                   srecv_sem, srrecv_sem, ssend_sem, srsend_sem, gsend_sem, grecv_sem):
@@ -63,7 +63,7 @@
     my_x = lax.rem(me // 2, side)
     my_y = me // (2 * side)
     e_local, rows_u, model = xb.shape
-    rows_s = dadb.shape[1]
+    rows_s = rows_u // (UNIT_BLOCKS // STEP_BLOCKS)
     ffn = hb.shape[2]
     cap = x_hbm.shape[2]
     tok = ag.shape[2]
@@ -75,6 +75,7 @@
     per_step = 2 * STEP_BLOCKS
     tile = 256
     mt_count = model // tile
+    dadb = wgu
     ft_count = ffn // tile
 
     def device(y, x, c):
@@ -146,20 +147,15 @@
     def unit_x(g, e):
         return [x_copy(g * UNIT_BLOCKS, j, e, 0, 0) for j in range(per_unit)]
 
-    def half_rows(t):
-        return pl.multiple_of(lax.rem(t, 2) * rows_s, rows_s)
-
-    def step_fill(t, e):
-        row = half_rows(t)
-        here, u = pl.ds(row, rows_s), (t // 2) * e_local + e
-        half = lax.rem(t, 2)
-        return ([x_copy(t * STEP_BLOCKS, j, e, row, half * per_step) for j in range(per_step)]
-                + [pltpu.make_async_copy(pq_hbm.at[u, here], pq.at[e, here], fill_sem.at[e, half, 0]),
-                   pltpu.make_async_copy(h_hbm.at[u, here], hb.at[e, here], fill_sem.at[e, half, 1])])
+    def unit_fill(g, e):
+        u = g * e_local + e
+        return unit_x(g, e) + [pltpu.make_async_copy(pq_hbm.at[u], pq.at[e], fill_sem.at[e, 0]),
+                               pltpu.make_async_copy(h_hbm.at[u], hb.at[e], fill_sem.at[e, 1])]
 
     def dadb_copy(t, e, j):
         src = origin(t * STEP_BLOCKS + j // 2, j % 2)
-        return pltpu.make_async_copy(dadb.at[e, pl.ds(j * cap, cap)], dadb_hbm.at[src, e], dadb_sem.at[e, j])
+        row = pl.multiple_of(lax.rem(t, 2) * rows_s + j * cap, cap)
+        return pltpu.make_async_copy(dadb.at[e, pl.ds(row, cap)], dadb_hbm.at[src, e], dadb_sem.at[e, j])
 
     def spill_copies(u, e):
         return (pltpu.make_async_copy(pq.at[e], pq_hbm.at[u], spill_sem.at[e, 0]),
@@ -249,10 +245,9 @@
     for e in range(e_local):
         for c in spill_copies((units - 1) * e_local + e, e):
             c.wait()
-    for t in range(2):
-        for e in range(e_local):
-            for c in step_fill(jnp.int32(t), e):
-                c.start()
+    for e in range(e_local):
+        for c in unit_fill(0, e):
+            c.start()
     w_copies[2].wait()
 
     def hits(r, p, e):
@@ -274,8 +269,10 @@
     @pl.loop(0, steps)
     def _(t):
         on(BEFORE, t)
-        half = half_rows(t)
+        odd = lax.rem(t, 2)
+        half = pl.multiple_of(odd * rows_s, rows_s)
         here = pl.ds(half, rows_s)
+        dy_here = pl.ds(pl.multiple_of(rows_s + half, rows_s), rows_s)
 
         @pl.loop(0, STEP_BLOCKS)
         def _(i):
@@ -298,61 +295,70 @@
                     for e in range(e_local):
                         d_e = d[e * cap:(e + 1) * cap]
                         db[e, pl.ds(row, cap), cols] = d_e.astype(BF16)
-                        db[e, pl.ds(rows_s + row, cap), cols] = (d_e * gates[e]).astype(BF16)
+                        db[e, pl.ds(pl.multiple_of(rows_s + half + row, cap), cap), cols] = (d_e * gates[e]).astype(BF16)
 
         @pl.loop(0, e_local)
         def _(e):
-            for c in step_fill(t, e):
-                c.wait()
+            @pl.when(odd == 0)
+            def _():
+                for c in unit_fill(t // 2, e):
+                    c.wait()
 
             @pl.when(t > 0)
             def _():
                 for j in range(per_step):
                     dadb_copy(t, e, j).wait()
 
-            gg[...] = jnp.zeros_like(gg)
-
-            @pl.loop(0, ft_count)
-            def _(n):
-                lo = pl.ds(pl.multiple_of(n * tile, tile), tile)
-                hi = pl.ds(pl.multiple_of(ffn + n * tile, tile), tile)
-                both = lax.dot_general(db[e], wd[e, lo, :], NT, preferred_element_type=F32)
+            part = jnp.zeros((rows_s, 128), F32)
+            for n in range(ft_count):
+                lo, hi = pl.ds(n * tile, tile), pl.ds(ffn + n * tile, tile)
+                lhs = jnp.concatenate([db[e, 0:rows_s], db[e, dy_here]], axis=0)
+                both = lax.dot_general(lhs, wd[e, lo, :], NT, preferred_element_type=F32)
                 prod = hb[e, here, lo].astype(F32) * both[:rows_s]
-                gg[...] += prod[:, :128] + prod[:, 128:]
+                part += prod[:, :128] + prod[:, 128:]
                 dh = both[rows_s:].astype(BF16).astype(F32)
-                dadb[e, :, lo] = (dh * pq[e, here, lo]).astype(BF16)
-                dadb[e, :, hi] = (dh * pq[e, here, hi]).astype(BF16)
-
-            for j in range(per_step):
-                dadb_copy(t, e, j).start()
-
-            total = jnp.broadcast_to(jnp.sum(gg[...], axis=1, keepdims=True), gg.shape)
+                dadb[e, here, lo] = (dh * pq[e, here, lo]).astype(BF16)
+                dadb[e, here, hi] = (dh * pq[e, here, hi]).astype(BF16)
+
+            total = jnp.broadcast_to(jnp.sum(part, axis=1, keepdims=True), part.shape)
             for j in range(per_step):
                 slot, _ = hits(j % 2, t * STEP_BLOCKS + j // 2, e)
                 value = jnp.concatenate([total[j * cap:(j + 1) * cap]] * (tok // 128), axis=1)
                 gsend[t * per_step + j, e] = jnp.sum(
                     jnp.where(slot_iota == slot, value, 0.0), axis=0, keepdims=True)
 
-            @pl.loop(0, model // 512)
-            def _(m):
-                rows = pl.ds(pl.multiple_of(m * 512, 512), 512)
-                for n in range(2):
-                    cols = pl.ds(n * ffn, ffn)
-                    acc_gu[e, rows, cols] += lax.dot_general(
-                        xb[e, here, rows], dadb[e, :, cols], TN, preferred_element_type=F32)
-
-            for n in range(model // 512):
-                cols = pl.ds(n * 512, 512)
-                acc_d[e, :, cols] += lax.dot_general(
-                    hb[e, here, :], db[e, rows_s:, cols], TN, preferred_element_type=F32)
-
-            @pl.when(t + 2 < steps)
+            for j in range(per_step):
+                dadb_copy(t, e, j).start()
+
+            def weight_grads(rows, dy_rows):
+                @pl.loop(0, 2)
+                def _(m):
+                    out = pl.ds(pl.multiple_of(m * (model // 2), model // 2), model // 2)
+                    for n in range(2):
+                        cols = pl.ds(n * ffn, ffn)
+                        acc_gu[e, out, cols] += lax.dot_general(
+                            xb[e, rows, out], dadb[e, rows, cols], TN, preferred_element_type=F32)
+
+                for n in range(model // 512):
+                    cols = pl.ds(n * 512, 512)
+                    acc_d[e, :, cols] += lax.dot_general(
+                        hb[e, rows, :], db[e, dy_rows, cols], TN, preferred_element_type=F32)
+
+            @pl.when((odd == 1) & (t < steps - 2))
             def _():
-                for c in step_fill(t + 2, e):
+                weight_grads(pl.ds(0, rows_u), pl.ds(rows_s, rows_u))
+                for c in unit_fill(t // 2 + 1, e):
                     c.start()
+
+            @pl.when(t >= steps - 2)
+            def _():
+                weight_grads(here, dy_here)
 
             @pl.when(t + 1 == steps)
             def _():
+                for j in range(per_step):
+                    dadb_copy(t, e, j).wait()
+
                 @pl.loop(0, mt_count)
                 def _(m):
                     rows = pl.ds(pl.multiple_of(m * tile, tile), tile)
@@ -384,10 +390,6 @@
             pltpu.make_async_remote_copy(
                 src_ref=gsend.at[t * per_step + j], dst_ref=grecv.at[me], send_sem=gsend_sem,
                 recv_sem=grecv_sem, device_id={'ep': to}, device_id_type=MESH).start()
-
-    for e in range(e_local):
-        for j in range(per_step):
-            dadb_copy(jnp.int32(steps - 1), e, j).wait()
 
     def drain(ref, sem):
         pltpu.make_async_copy(ref, ref, sem).wait()
@@ -434,14 +436,12 @@
         pltpu.VMEM((e_local, model, 2 * ffn), BF16),
         pltpu.VMEM((e_local, ffn, model), BF16),
         pltpu.VMEM((e_local, rows_u, model), BF16),
-        pltpu.VMEM((e_local, 2 * rows_s, model), BF16),
+        pltpu.VMEM((e_local, rows_s + rows_u, model), BF16),
         pltpu.VMEM((e_local, rows_u, 2 * ffn), F32),
         pltpu.VMEM((e_local, rows_u, ffn), BF16),
-        pltpu.VMEM((e_local, rows_s, 2 * ffn), BF16),
-        pltpu.VMEM((rows_s, 128), F32),
         pltpu.VMEM((group_size, e_local, 1, tok), F32),
         pltpu.VMEM((group_size, e_local, 1, tok), F32),
-        dma((3,)), dma((2,)), dma((e_local, per_unit)), dma((e_local, 2)), dma((e_local, 2, 2)),
+        dma((3,)), dma((2,)), dma((e_local, per_unit)), dma((e_local, 2)), dma((e_local, 2)),
         dma((e_local, per_step)), dma((e_local, 2)),
         dma((n_blocks, QUARTERS)), dma((n_blocks,)), dma, dma,
         dma((n_blocks, QUARTERS)), dma((n_blocks,)), dma, dma, dma, dma,

time: 130 us -> 122 us (0.938)
  Pallas kernels: 124 us -> 117 us
    pallas_call x1, Pallas kernels: 104 us -> 96.6 us  [run_experts(): pl.pallas_call(functools.partial(expert_kernel, group_size), out_shape=ou...]
where the time goes in v3:
time: 122 us
  Pallas kernels  117 us (96%)
  other arithmetic  2.63 us (2%)
  local copies, waits for them, and re-layouts  1.29 us (1%)
    pallas_call x1, Pallas kernels, run_experts(): pl.pallas_call(functools.partial(expert_kernel, group_size), out_shape=ou...  96.6 us
    pallas_call x1, Pallas kernels, run_finish(): pl.pallas_call(functools.partial(finish_kernel, group_size), grid=(e_loca...  20.4 us

profile of v3, /device:TPU:97, one launch (start us, length us, event | category | flops | bytes accessed | tf_op | source)
XLA Modules:
  0.0 121.6 jit_solution(6483010587811572759)
XLA Ops:
  0.6 1.3 %fusion = (s32[8,256]{1,0:T(8,128)}, f32[8,256]{1,0:T(8,128)S(1)}, s32[8,256]{1,0:T(8,128)}) fusion(s32[6,256]{1,0:T(8,128)} %bitcast.5, s32[6,256]{1,0:T(8,128)} %bitcast.6), kind=kLoop, calls=%fused_computation.4 | loop fusion | flops 10240 | bytes 36864 | tf_op jit(solution)/shard_map/jit(_pad)/pad | solution.py:522
  2.0 1.3 %select_maximum_fusion.route_hbm = f32[16,256]{1,0:T(8,128)} fusion(f32[6,256]{1,0:T(8,128)} %bitcast.7, f32[8,256]{1,0:T(8,128)S(1)} %get-tuple-element.24), kind=kLoop, calls=%fused_computation | loop fusion | flops 12288 | bytes 30720 | tf_op jit(solution)/shard_map/concatenate | solution.py:525
  3.3 96.6 %shard_map.119 = (bf16[32,2,48,1024]{3,2,1,0:T(8,128)(2,1)}, bf16[2,1536,1024]{2,1,0:T(8,128)(2,1)}, bf16[2,512,1536]{2,1,0:T(8,128)(2,1)}, f32[32,2,1,256]{3,2,...) custom-call(bf16[32,2,48,1536]{3,2,1,0:T(8,128)(2,1)} %x_hbm.1, bf16[2,1536,512]{2,1,0:T(8,128)(2,1)} %wg.1, ...), custom_call_target="tpu_custom_call" | custom-call | tf_op jit(solution)/shard_map/pallas_call | solution.py:449
  99.9 20.4 %shard_map.120 = (bf16[32,2,48,1536]{3,2,1,0:T(8,128)(2,1)}, bf16[2,1536,512]{2,1,0:T(8,128)(2,1)}, bf16[2,1536,512]{2,1,0:T(8,128)(2,1)}, bf16[2,512,1536]{2,1,0:T(8,128)(2,1)}, f32[8,256]{1,0:T(8,128)}) custom-call(bf16[32,2,48,1024]{3,2,1,0:T(8,128)(2,1)} %get-tuple-element.14.dadb, bf16[2,1536,512]{2,1,0:T(8,128)(2,1)} %wg.1, bf16[2,1536,512]{2,1,0:T(8,128)(2,1)} %wu.1, ...), custom_call_target="tpu_custom_call" | custom-call | tf_op jit(solution)/shard_map/pallas_call | solution.py:487
  120.3 1.3 %slice_bitcast_fusion = f32[256,6]{0,1:T(8,128)} fusion(f32[8,256]{1,0:T(8,128)} %get-tuple-element.22), kind=kLoop, calls=%fused_computation.2 | loop fusion | bytes 12288 | tf_op jit(solution)/shard_map/transpose | solution.py:529

commit v4 on v3

--- a/solution.py
+++ b/solution.py
@@ -24,6 +24,8 @@
 
 ORIGIN_Y, ORIGIN_X = packed([b[0] for b in ORDER]), packed([b[1] for b in ORDER])
 QUARTERS = 4
+VMEM_A = 45 * 1024 * 1024 + 900 * 1024
+VMEM_B = 40 * 1024 * 1024
 UNIT_BLOCKS = 4
 STEP_BLOCKS = 2
 BEFORE = {0: (3,), 3: (7,), 4: (9, 10), 6: (13,)}
@@ -51,10 +53,10 @@
 SLOTS = len(SENDS[(0, 1)])
 
 
-def expert_kernel(group_size, x_hbm, wg_hbm, wu_hbm, wd_hbm, dout_hbm, route_hbm,
-                  dadb_hbm, gu_hbm, dn_hbm, back_hbm, pq_hbm, h_hbm,
-                  ag, rt, acc_gu, acc_d, wgu, wd, xb, db, pq, hb, gsend, grecv,
-                  w_sem, own_sem, x_sem, spill_sem, fill_sem, dadb_sem, fin_sem,
+def expert_kernel(group_size, x_hbm, wg_hbm, wu_hbm, wd_hbm, dout_hbm, slots_ref, ids_ref, gates_ref,
+                  dadb_hbm, acc_gu, acc_d, back_hbm, pq_hbm, h_hbm,
+                  ag, rt, wgu, wd, xb, db, pq, hb, gsend, grecv,
+                  w_sem, own_sem, x_sem, spill_sem, fill_sem, dadb_sem,
                   recv_sem, rrecv_sem, send_sem, rsend_sem,
                   srecv_sem, srrecv_sem, ssend_sem, srsend_sem, gsend_sem, grecv_sem):
     side = math.isqrt(group_size // 2)
@@ -164,11 +166,9 @@
     w_copies = [pltpu.make_async_copy(wg_hbm, wgu.at[:, :, pl.ds(0, ffn)], w_sem.at[0]),
                 pltpu.make_async_copy(wu_hbm, wgu.at[:, :, pl.ds(ffn, ffn)], w_sem.at[1]),
                 pltpu.make_async_copy(wd_hbm, wd, w_sem.at[2])]
-    own = [pltpu.make_async_copy(dout_hbm, ag.at[0, 0], own_sem.at[0]),
-           pltpu.make_async_copy(route_hbm, rt.at[0, 0], own_sem.at[1])]
-
-    for c in own:
-        c.start()
+    own = pltpu.make_async_copy(dout_hbm, ag.at[0, 0], own_sem)
+
+    own.start()
     barrier = pltpu.get_barrier_semaphore()
 
     @pl.loop(1, group_size)
@@ -181,8 +181,12 @@
         for c in unit_x(0, e):
             c.start()
     w_copies[2].start()
-    for c in own:
-        c.wait()
+    top_k = slots_ref.shape[0]
+    rt[0, 0] = jnp.concatenate([jnp.full((8, tok), -1.0, F32), jnp.zeros((8, tok), F32)], axis=0)
+    slots = slots_ref[...]
+    rt[0, 0, 0:top_k] = jnp.where(slots >= 0, ids_ref[...] * cap + slots, -1).astype(F32)
+    rt[0, 0, 8:8 + top_k] = gates_ref[...]
+    own.wait()
     pl.semaphore_wait(barrier, group_size - 1)
     for slot in range(3):
         issue(slot)
@@ -354,24 +358,6 @@
             def _():
                 weight_grads(here, dy_here)
 
-            @pl.when(t + 1 == steps)
-            def _():
-                for j in range(per_step):
-                    dadb_copy(t, e, j).wait()
-
-                @pl.loop(0, mt_count)
-                def _(m):
-                    rows = pl.ds(pl.multiple_of(m * tile, tile), tile)
-                    wgu[e, rows] = acc_gu[e, rows].astype(BF16)
-
-                @pl.loop(0, ft_count)
-                def _(m):
-                    rows = pl.ds(pl.multiple_of(m * tile, tile), tile)
-                    wd[e, rows] = acc_d[e, rows].astype(BF16)
-
-                pltpu.make_async_copy(wgu.at[e], gu_hbm.at[e], fin_sem.at[e, 0]).start()
-                pltpu.make_async_copy(wd.at[e], dn_hbm.at[e], fin_sem.at[e, 1]).start()
-
             for step, slots in BETWEEN.items():
                 @pl.when((t == step) & (e == 0))
                 def _(slots=slots):
@@ -400,15 +386,15 @@
     drain(rt.at[0], srsend_sem)
     drain(gsend.at[pl.ds(0, group_size - 1)], gsend_sem)
     drain(grecv.at[pl.ds(0, group_size - 1)], grecv_sem)
-    back = pltpu.make_async_copy(grecv, back_hbm, own_sem.at[0])
+    back = pltpu.make_async_copy(grecv, back_hbm, own_sem)
     back.start()
+    for e in range(e_local):
+        for j in range(per_step):
+            dadb_copy(jnp.int32(steps - 1), e, j).wait()
     back.wait()
-    for e in range(e_local):
-        pltpu.make_async_copy(wgu.at[e], gu_hbm.at[e], fin_sem.at[e, 0]).wait()
-        pltpu.make_async_copy(wd.at[e], dn_hbm.at[e], fin_sem.at[e, 1]).wait()
-
-
-def run_experts(x_disp, w_gate, w_up, w_down, d_out, route, group_size):
+
+
+def run_experts(x_disp, w_gate, w_up, w_down, d_out, slots, ids, gates, group_size):
     sources, e_local, cap, model = x_disp.shape
     ffn = w_gate.shape[2]
     tok = d_out.shape[0]
@@ -420,10 +406,11 @@
     units = n_blocks // UNIT_BLOCKS * e_local
     dma = pltpu.SemaphoreType.DMA
     any_spec = pl.BlockSpec(memory_space=pl.ANY)
+    vmem_spec = pl.BlockSpec(memory_space=pltpu.VMEM)
     out_shape = [
         jax.ShapeDtypeStruct((sources, e_local, cap, 2 * ffn), BF16),
-        jax.ShapeDtypeStruct((e_local, model, 2 * ffn), BF16),
-        jax.ShapeDtypeStruct((e_local, ffn, model), BF16),
+        pltpu.VMEM((e_local, model, 2 * ffn), F32),
+        pltpu.VMEM((e_local, ffn, model), F32),
         jax.ShapeDtypeStruct((group_size, e_local, 1, tok), F32),
         jax.ShapeDtypeStruct((units, rows_u, 2 * ffn), F32),
         jax.ShapeDtypeStruct((units, rows_u, ffn), BF16),
@@ -431,8 +418,6 @@
     scratch = [
         pltpu.VMEM((2, n_blocks, tok, model), BF16),
         pltpu.VMEM((2, n_blocks, 16, tok), F32),
-        pltpu.VMEM((e_local, model, 2 * ffn), F32),
-        pltpu.VMEM((e_local, ffn, model), F32),
         pltpu.VMEM((e_local, model, 2 * ffn), BF16),
         pltpu.VMEM((e_local, ffn, model), BF16),
         pltpu.VMEM((e_local, rows_u, model), BF16),
@@ -441,92 +426,147 @@
         pltpu.VMEM((e_local, rows_u, ffn), BF16),
         pltpu.VMEM((group_size, e_local, 1, tok), F32),
         pltpu.VMEM((group_size, e_local, 1, tok), F32),
-        dma((3,)), dma((2,)), dma((e_local, per_unit)), dma((e_local, 2)), dma((e_local, 2)),
-        dma((e_local, per_step)), dma((e_local, 2)),
+        dma((3,)), dma, dma((e_local, per_unit)), dma((e_local, 2)), dma((e_local, 2)),
+        dma((e_local, per_step)),
         dma((n_blocks, QUARTERS)), dma((n_blocks,)), dma, dma,
         dma((n_blocks, QUARTERS)), dma((n_blocks,)), dma, dma, dma, dma,
     ]
     return pl.pallas_call(
         functools.partial(expert_kernel, group_size),
-        out_shape=out_shape, in_specs=[any_spec] * 6, out_specs=[any_spec] * 6, scratch_shapes=scratch,
-        compiler_params=pltpu.CompilerParams(collective_id=0, has_side_effects=True, vmem_limit_bytes=67043328),
-    )(x_disp, w_gate, w_up, w_down, d_out, route)
-
-
-def finish_kernel(group_size, dadb, wg, wu, gu, dn, back, ids, slots, gx, gg_w, gu_w, gd_w, gate_out):
-    sources, _, cap, width = dadb.shape
+        out_shape=out_shape, in_specs=[any_spec] * 5 + [vmem_spec] * 3,
+        out_specs=[any_spec, vmem_spec, vmem_spec, any_spec, any_spec, any_spec], scratch_shapes=scratch,
+        compiler_params=pltpu.CompilerParams(collective_id=0, has_side_effects=True, vmem_limit_bytes=VMEM_A),
+    )(x_disp, w_gate, w_up, w_down, d_out, slots, ids, gates)
+
+
+def finish_kernel(group_size, chunk, dadb, wg, wu, acc_gu, acc_d, back, ids, slots,
+                  gx, g_gate, g_up, g_down, gate_out,
+                  wbuf, dbuf, obuf, st_g, st_u, st_d, w_sem, d_sem, o_sem, s_sem):
+    sources, e_local, cap, width = dadb.shape
     ffn = width // 2
     model = gx.shape[3]
-    both = dadb[...].reshape(sources * cap, width)
-    for n in range(model // 512):
-        rows = pl.ds(n * 512, 512)
-        out = (lax.dot_general(both[:, :ffn], wg[0, rows], NT, preferred_element_type=F32)
-               + lax.dot_general(both[:, ffn:], wu[0, rows], NT, preferred_element_type=F32))
-        gx[:, 0, :, rows] = out.astype(BF16).reshape(sources, cap, 512)
-    gg_w[...] = gu[:, :, :ffn]
-    gu_w[...] = gu[:, :, ffn:]
-    gd_w[...] = dn[...]
-
-    @pl.when((pl.program_id(0) == 0) & (pl.program_id(1) == 0))
-    def _():
-        e_local = back.shape[1]
-        total = jnp.zeros(gate_out.shape, F32)
-        for d in range(group_size):
-            for e in range(e_local):
-                total += jnp.where(ids[...] == d * e_local + e, back[d, e], 0.0)
-        gate_out[...] = jnp.where(slots[...] >= 0, total, 0.0)
-
-
-def run_finish(dadb, w_gate, w_up, gu, dn, back, ids, slots, group_size):
+    per_e = sources // chunk
+    chunks = e_local * per_e
+    m_blk, f_blk = model // per_e, ffn // per_e
+    depth = dbuf.shape[0]
+
+    def load(c):
+        slot = lax.rem(c, depth)
+        return pltpu.make_async_copy(
+            dadb.at[pl.ds(lax.rem(c, per_e) * chunk, chunk), c // per_e], dbuf.at[slot], d_sem.at[slot])
+
+    def store(c):
+        slot = lax.rem(c, 2)
+        return pltpu.make_async_copy(
+            obuf.at[slot], gx.at[pl.ds(lax.rem(c, per_e) * chunk, chunk), c // per_e], o_sem.at[slot])
+
+    def weights(e):
+        return [pltpu.make_async_copy(wg.at[e], wbuf.at[e, :, pl.ds(0, ffn)], w_sem.at[e, 0]),
+                pltpu.make_async_copy(wu.at[e], wbuf.at[e, :, pl.ds(ffn, ffn)], w_sem.at[e, 1])]
+
+    def staged(c):
+        e, i = c // per_e, lax.rem(c, per_e)
+        m = pl.ds(pl.multiple_of(i * m_blk, m_blk), m_blk)
+        f = pl.ds(pl.multiple_of(i * f_blk, f_blk), f_blk)
+        return e, m, f, [pltpu.make_async_copy(st_g.at[e, m], g_gate.at[e, m], s_sem.at[c, 0]),
+                         pltpu.make_async_copy(st_u.at[e, m], g_up.at[e, m], s_sem.at[c, 1]),
+                         pltpu.make_async_copy(st_d.at[e, f], g_down.at[e, f], s_sem.at[c, 2])]
+
+    for c in weights(0):
+        c.start()
+    for k in range(depth):
+        load(jnp.int32(k)).start()
+    for e in range(1, e_local):
+        for c in weights(e):
+            c.start()
+
+    total = jnp.zeros(gate_out.shape, F32)
+    for d in range(group_size):
+        for e in range(e_local):
+            total += jnp.where(ids[...] == d * e_local + e, back[d, e], 0.0)
+    gate_out[...] = jnp.where(slots[...] >= 0, total, 0.0)
+
+    @pl.loop(0, chunks)
+    def _(c):
+        e, m, f, copies = staged(c)
+
+        @pl.when(lax.rem(c, per_e) == 0)
+        def _():
+            for w in weights(e):
+                w.wait()
+
+        load(c).wait()
+
+        @pl.when(c >= 2)
+        def _():
+            store(c - 2).wait()
+
+        slot, out_slot = lax.rem(c, depth), lax.rem(c, 2)
+        st_g[e, m] = acc_gu[e, m, 0:ffn].astype(BF16)
+        st_u[e, m] = acc_gu[e, m, ffn:width].astype(BF16)
+        st_d[e, f] = acc_d[e, f].astype(BF16)
+        both = dbuf[slot].reshape(chunk * cap, width)
+        for n in range(model // 512):
+            rows = pl.ds(n * 512, 512)
+            out = lax.dot_general(both, wbuf[e, rows], NT, preferred_element_type=F32)
+            obuf[out_slot, :, :, rows] = out.astype(BF16).reshape(chunk, cap, 512)
+        store(c).start()
+        for s in copies:
+            s.start()
+
+        @pl.when(c + depth < chunks)
+        def _():
+            load(c + depth).start()
+
+    for c in range(chunks - 2, chunks):
+        store(jnp.int32(c)).wait()
+    for c in range(chunks):
+        for s in staged(jnp.int32(c))[3]:
+            s.wait()
+
+
+def run_finish(dadb, w_gate, w_up, acc_gu, acc_d, back, ids, slots, group_size):
     sources, e_local, cap, width = dadb.shape
     model, ffn = w_gate.shape[1:]
-    steps = 4
-    s_blk, m_blk, f_blk = sources // steps, model // steps, ffn // steps
-    tok = ids.shape[1]
-    whole = lambda shape: pl.BlockSpec(shape, lambda e, i: (0,) * len(shape))
+    top_k, tok = ids.shape
+    chunk = 8
+    dma = pltpu.SemaphoreType.DMA
+    any_spec = pl.BlockSpec(memory_space=pl.ANY)
+    vmem_spec = pl.BlockSpec(memory_space=pltpu.VMEM)
     return pl.pallas_call(
-        functools.partial(finish_kernel, group_size),
-        grid=(e_local, steps),
-        in_specs=[
-            pl.BlockSpec((s_blk, 1, cap, width), lambda e, i: (i, e, 0, 0)),
-            pl.BlockSpec((1, model, ffn), lambda e, i: (e, 0, 0)),
-            pl.BlockSpec((1, model, ffn), lambda e, i: (e, 0, 0)),
-            pl.BlockSpec((1, m_blk, width), lambda e, i: (e, i, 0)),
-            pl.BlockSpec((1, f_blk, model), lambda e, i: (e, i, 0)),
-            whole(back.shape), whole((8, tok)), whole((8, tok)),
-        ],
-        out_specs=[
-            pl.BlockSpec((s_blk, 1, cap, model), lambda e, i: (i, e, 0, 0)),
-            pl.BlockSpec((1, m_blk, ffn), lambda e, i: (e, i, 0)),
-            pl.BlockSpec((1, m_blk, ffn), lambda e, i: (e, i, 0)),
-            pl.BlockSpec((1, f_blk, model), lambda e, i: (e, i, 0)),
-            whole((8, tok)),
-        ],
+        functools.partial(finish_kernel, group_size, chunk),
+        in_specs=[any_spec] * 3 + [vmem_spec] * 5,
+        out_specs=[any_spec] * 4 + [vmem_spec],
         out_shape=[
             jax.ShapeDtypeStruct((sources, e_local, cap, model), BF16),
             jax.ShapeDtypeStruct((e_local, model, ffn), BF16),
             jax.ShapeDtypeStruct((e_local, model, ffn), BF16),
             jax.ShapeDtypeStruct((e_local, ffn, model), BF16),
-            jax.ShapeDtypeStruct((8, tok), F32),
+            jax.ShapeDtypeStruct((top_k, tok), F32),
         ],
-    )(dadb, w_gate, w_up, gu, dn, back, ids, slots)
+        scratch_shapes=[
+            pltpu.VMEM((e_local, model, width), BF16),
+            pltpu.VMEM((3, chunk, cap, width), BF16),
+            pltpu.VMEM((2, chunk, cap, model), BF16),
+            pltpu.VMEM((e_local, model, ffn), BF16),
+            pltpu.VMEM((e_local, model, ffn), BF16),
+            pltpu.VMEM((e_local, ffn, model), BF16),
+            dma((e_local, 2)), dma((3,)), dma((2,)), dma((e_local * sources // chunk, 3)),
+        ],
+        compiler_params=pltpu.CompilerParams(vmem_limit_bytes=VMEM_B),
+    )(dadb, w_gate, w_up, acc_gu, acc_d, back, ids, slots)
 
 
 def solution(mesh):
     group_size = mesh.shape['ep']
 
     def local_step(x_disp, w_gate, w_up, w_down, d_out, slot_idx, expert_id, gate_wt):
-        cap = x_disp.shape[2]
-        top_k = slot_idx.shape[1]
-        pad = ((0, 8 - top_k), (0, 0))
-        slots = jnp.pad(slot_idx.T, pad, constant_values=-1)
-        ids = jnp.pad(expert_id.T, pad)
-        pos = jnp.where(slots >= 0, ids * cap + slots, -1).astype(F32)
-        route = jnp.concatenate([pos, jnp.pad(gate_wt.T, pad)], axis=0)
-        dadb, gu, dn, back, _, _ = run_experts(x_disp, w_gate, w_up, w_down, d_out, route, group_size)
+        slots, ids = slot_idx.T, expert_id.T
+        dadb, acc_gu, acc_d, back, _, _ = run_experts(
+            x_disp, w_gate, w_up, w_down, d_out, slots, ids, gate_wt.T, group_size)
         grad_x, grad_w_gate, grad_w_up, grad_w_down, gate = run_finish(
-            dadb, w_gate, w_up, gu, dn, back, ids, slots, group_size)
-        return grad_x, grad_w_gate, grad_w_up, grad_w_down, gate[:top_k].T
+            dadb, w_gate, w_up, acc_gu, acc_d, back, ids, slots, group_size)
+        return grad_x, grad_w_gate, grad_w_up, grad_w_down, gate.T
 
     token_place = P(('dp', 'ep'), None)
     weight_place = P('ep', None, None)

time: 122 us -> 134 us (1.098)
  local copies, waits for them, and re-layouts: 1.29 us -> 14.5 us
  other arithmetic: 2.63 us -> 0 us
    unnamed x0 -> x16, local copies, waits for them, and re-layouts: none -> 14.5 us
    pallas_call x1, Pallas kernels: 20.4 us -> 22 us  [run_finish(): pl.pallas_call(functools.partial(finish_kernel, group_size, chunk), in_sp...]
where the time goes in v4:
time: 134 us
  Pallas kernels  118 us (88%)
  local copies, waits for them, and re-layouts  14.5 us (11%)
    pallas_call x1, Pallas kernels, run_experts(): pl.pallas_call(functools.partial(expert_kernel, group_size), out_shape=ou...  96.4 us
    pallas_call x1, Pallas kernels, run_finish(): pl.pallas_call(functools.partial(finish_kernel, group_size, chunk), in_sp...  22 us
    unnamed x16, local copies, waits for them, and re-layouts  14.5 us

profile of v4, /device:TPU:97, one launch (start us, length us, event | category | flops | bytes accessed | tf_op | source)
XLA Modules:
  0.0 133.6 jit_solution(12234790576232130641)
XLA Ops:
  0.6 0.0 copy-start.6
  0.6 0.0 copy-start.7
  0.7 96.4 %shard_map.119 = (bf16[32,2,48,1024]{3,2,1,0:T(8,128)(2,1)}, f32[2,1536,1024]{2,1,0:T(8,128)S(1)}, f32[2,512,1536]{2,1,0:T(8,128)S(1)}, f32[32,2,1,256]{3,2,1,0:...) custom-call(bf16[32,2,48,1536]{3,2,1,0:T(8,128)(2,1)} %x_hbm.1, bf16[2,1536,512]{2,1,0:T(8,128)(2,1)} %wg.1, ...), custom_call_target="tpu_custom_call" | custom-call | tf_op jit(solution)/shard_map/pallas_call | solution.py:434
  97.0 0.0 copy-start
  97.0 4.5 %copy-done = f32[2,1536,1024]{2,1,0:T(8,128)} copy-done((f32[2,1536,1024]{2,1,0:T(8,128)}, f32[2,1536,1024]{2,1,0:T(8,128)S(1)}, u32[]{:S(2)}) %copy-start) | copy-done | bytes 12582936
  101.5 0.0 copy-start.4
  101.5 2.6 %copy-done.4 = f32[2,512,1536]{2,1,0:T(8,128)} copy-done((f32[2,512,1536]{2,1,0:T(8,128)}, f32[2,512,1536]{2,1,0:T(8,128)S(1)}, u32[]{:S(2)}) %copy-start.4) | copy-done | bytes 6291480
  104.1 0.0 copy-done.6
  104.1 0.0 copy-done.7
  104.2 0.0 copy-start.1
  104.2 1.9 %copy-done.1 = bf16[2,1536,512]{2,1,0:T(8,128)(2,1)S(1)} copy-done((bf16[2,1536,512]{2,1,0:T(8,128)(2,1)S(1)}, bf16[2,1536,512]{2,1,0:T(8,128)(2,1)}, u32[]{:S(2)}) %copy-start.1) | copy-done | bytes 3145752
  106.0 0.0 copy-start.2
  106.0 1.9 %copy-done.2 = bf16[2,1536,512]{2,1,0:T(8,128)(2,1)S(1)} copy-done((bf16[2,1536,512]{2,1,0:T(8,128)(2,1)S(1)}, bf16[2,1536,512]{2,1,0:T(8,128)(2,1)}, u32[]{:S(2)}) %copy-start.2) | copy-done | bytes 3145752
  107.9 0.0 copy-start.3
  107.9 2.8 %copy-done.3 = bf16[32,2,48,1024]{3,2,1,0:T(8,128)(2,1)S(1)} copy-done((bf16[32,2,48,1024]{3,2,1,0:T(8,128)(2,1)S(1)}, bf16[32,2,48,1024]{3,2,1,0:T(8,128)(2,1)}, u32[]{:S(2)}) %copy-start.3) | copy-done | bytes 6291480
  110.7 0.0 copy-start.5
  110.7 0.8 copy-done.5
  111.6 22.0 %shard_map.120 = (bf16[32,2,48,1536]{3,2,1,0:T(8,128)(2,1)}, bf16[2,1536,512]{2,1,0:T(8,128)(2,1)}, bf16[2,1536,512]{2,1,0:T(8,128)(2,1)}, bf16[2,512,1536]{2,1,0:T(8,128)(2,1)}, f32[6,256]{1,0:T(8,128)}) custom-call(bf16[32,2,48,1024]{3,2,1,0:T(8,128)(2,1)S(1)} %copy-done.3, bf16[2,1536,512]{2,1,0:T(8,128)(2,1)S(1)} %copy-done.1, ...), custom_call_target="tpu_custom_call" | custom-call | tf_op jit(solution)/shard_map/pallas_call | solution.py:536
Async XLA Ops:
  0.6 103.5 %copy-start.6 = (s32[256,6]{0,1:T(8,128)S(1)}, s32[256,6]{0,1:T(8,128)}, u32[]{:S(2)}) copy-start(s32[256,6]{0,1:T(8,128)} %param.13) | copy-start | bytes 18436
  0.6 103.5 %copy-start.7 = (s32[256,6]{0,1:T(8,128)S(1)}, s32[256,6]{0,1:T(8,128)}, u32[]{:S(2)}) copy-start(s32[256,6]{0,1:T(8,128)} %param.14) | copy-start | bytes 18436
  97.0 4.5 %copy-start = (f32[2,1536,1024]{2,1,0:T(8,128)}, f32[2,1536,1024]{2,1,0:T(8,128)S(1)}, u32[]{:S(2)}) copy-start(f32[2,1536,1024]{2,1,0:T(8,128)S(1)} %get-tuple-element.15.acc_gu) | copy-start | bytes 37748740
  101.5 2.6 %copy-start.4 = (f32[2,512,1536]{2,1,0:T(8,128)}, f32[2,512,1536]{2,1,0:T(8,128)S(1)}, u32[]{:S(2)}) copy-start(f32[2,512,1536]{2,1,0:T(8,128)S(1)} %get-tuple-element.16.acc_d) | copy-start | bytes 18874372
  104.2 1.9 %copy-start.1 = (bf16[2,1536,512]{2,1,0:T(8,128)(2,1)S(1)}, bf16[2,1536,512]{2,1,0:T(8,128)(2,1)}, u32[]{:S(2)}) copy-start(bf16[2,1536,512]{2,1,0:T(8,128)(2,1)} %wg.1) | copy-start | bytes 9437188
  106.0 1.9 %copy-start.2 = (bf16[2,1536,512]{2,1,0:T(8,128)(2,1)S(1)}, bf16[2,1536,512]{2,1,0:T(8,128)(2,1)}, u32[]{:S(2)}) copy-start(bf16[2,1536,512]{2,1,0:T(8,128)(2,1)} %wu.1) | copy-start | bytes 9437188
  107.9 2.8 %copy-start.3 = (bf16[32,2,48,1024]{3,2,1,0:T(8,128)(2,1)S(1)}, bf16[32,2,48,1024]{3,2,1,0:T(8,128)(2,1)}, u32[]{:S(2)}) copy-start(bf16[32,2,48,1024]{3,2,1,0:T(8,128)(2,1)} %get-tuple-element.14.dadb) | copy-start | bytes 18874372
  110.7 0.8 copy-start.5

commit v5 on v4

--- a/solution.py
+++ b/solution.py
@@ -25,11 +25,11 @@
 ORIGIN_Y, ORIGIN_X = packed([b[0] for b in ORDER]), packed([b[1] for b in ORDER])
 QUARTERS = 4
 VMEM_A = 45 * 1024 * 1024 + 900 * 1024
-VMEM_B = 40 * 1024 * 1024
+VMEM_B = 22 * 1024 * 1024
 UNIT_BLOCKS = 4
 STEP_BLOCKS = 2
-BEFORE = {0: (3,), 3: (7,), 4: (9, 10), 6: (13,)}
-BETWEEN = {0: (4,), 1: (5,), 2: (6,), 3: (8,), 4: (11,), 5: (12,)}
+BEFORE = {0: (3,), 3: (7,), 4: (8, 9, 10), 6: (13,)}
+BETWEEN = {0: (4,), 1: (5,), 2: (6,), 4: (11,), 5: (12,)}
 AFTER = {6: (14,)}
 NT = (((1,), (1,)), ((), ()))
 TN = (((0,), (0,)), ((), ()))
@@ -439,9 +439,9 @@
     )(x_disp, w_gate, w_up, w_down, d_out, slots, ids, gates)
 
 
-def finish_kernel(group_size, chunk, dadb, wg, wu, acc_gu, acc_d, back, ids, slots,
+def finish_kernel(group_size, chunk, dadb, wg, wu, back_hbm, acc_gu, acc_d, ids, slots,
                   gx, g_gate, g_up, g_down, gate_out,
-                  wbuf, dbuf, obuf, st_g, st_u, st_d, w_sem, d_sem, o_sem, s_sem):
+                  wbuf, dbuf, obuf, st_g, st_u, st_d, back, w_sem, d_sem, o_sem, s_sem, b_sem):
     sources, e_local, cap, width = dadb.shape
     ffn = width // 2
     model = gx.shape[3]
@@ -480,11 +480,8 @@
         for c in weights(e):
             c.start()
 
-    total = jnp.zeros(gate_out.shape, F32)
-    for d in range(group_size):
-        for e in range(e_local):
-            total += jnp.where(ids[...] == d * e_local + e, back[d, e], 0.0)
-    gate_out[...] = jnp.where(slots[...] >= 0, total, 0.0)
+    back_copy = pltpu.make_async_copy(back_hbm, back, b_sem)
+    back_copy.start()
 
     @pl.loop(0, chunks)
     def _(c):
@@ -518,6 +515,13 @@
         def _():
             load(c + depth).start()
 
+    back_copy.wait()
+    total = jnp.zeros(gate_out.shape, F32)
+    for d in range(group_size):
+        for e in range(e_local):
+            total += jnp.where(ids[...] == d * e_local + e, back[d, e], 0.0)
+    gate_out[...] = jnp.where(slots[...] >= 0, total, 0.0)
+
     for c in range(chunks - 2, chunks):
         store(jnp.int32(c)).wait()
     for c in range(chunks):
@@ -535,7 +539,7 @@
     vmem_spec = pl.BlockSpec(memory_space=pltpu.VMEM)
     return pl.pallas_call(
         functools.partial(finish_kernel, group_size, chunk),
-        in_specs=[any_spec] * 3 + [vmem_spec] * 5,
+        in_specs=[any_spec] * 4 + [vmem_spec] * 4,
         out_specs=[any_spec] * 4 + [vmem_spec],
         out_shape=[
             jax.ShapeDtypeStruct((sources, e_local, cap, model), BF16),
@@ -551,10 +555,12 @@
             pltpu.VMEM((e_local, model, ffn), BF16),
             pltpu.VMEM((e_local, model, ffn), BF16),
             pltpu.VMEM((e_local, ffn, model), BF16),
-            dma((e_local, 2)), dma((3,)), dma((2,)), dma((e_local * sources // chunk, 3)),
+            pltpu.VMEM(back.shape, F32),
+            dma((e_local, 2)), dma((3,)), dma((2,)), dma((e_local * sources // chunk, 3)), dma,
         ],
         compiler_params=pltpu.CompilerParams(vmem_limit_bytes=VMEM_B),
-    )(dadb, w_gate, w_up, acc_gu, acc_d, back, ids, slots)
+    )(*[pltpu.with_memory_space_constraint(a, pltpu.HBM) for a in (dadb, w_gate, w_up, back)],
+      *[pltpu.with_memory_space_constraint(a, pltpu.VMEM) for a in (acc_gu, acc_d)], ids, slots)
 
 
 def solution(mesh):

time: 134 us -> 114 us (0.85)
  local copies, waits for them, and re-layouts: 14.5 us -> 0.01 us
  Pallas kernels: 118 us -> 113 us
    unnamed x16 -> x4, local copies, waits for them, and re-layouts: 14.5 us -> 0.01 us
    pallas_call x1, Pallas kernels: 22 us -> 16.1 us  [run_finish(): pl.pallas_call(functools.partial(finish_kernel, group_size, chunk), in_sp...]
where the time goes in v5:
time: 114 us
  Pallas kernels  113 us (99%)
    pallas_call x1, Pallas kernels, run_experts(): pl.pallas_call(functools.partial(expert_kernel, group_size), out_shape=ou...  97 us
    pallas_call x1, Pallas kernels, run_finish(): pl.pallas_call(functools.partial(finish_kernel, group_size, chunk), in_sp...  16.1 us

profile of v5, /device:TPU:97, one launch (start us, length us, event | category | flops | bytes accessed | tf_op | source)
XLA Modules:
  0.0 113.8 jit_solution(362390745332997229)
XLA Ops:
  0.6 0.0 copy-start
  0.6 0.0 copy-start.1
  0.7 97.0 %shard_map.119 = (bf16[32,2,48,1024]{3,2,1,0:T(8,128)(2,1)}, f32[2,1536,1024]{2,1,0:T(8,128)S(1)}, f32[2,512,1536]{2,1,0:T(8,128)S(1)}, f32[32,2,1,256]{3,2,1,0:...) custom-call(bf16[32,2,48,1536]{3,2,1,0:T(8,128)(2,1)} %x_hbm.1, bf16[2,1536,512]{2,1,0:T(8,128)(2,1)} %wg.1, ...), custom_call_target="tpu_custom_call" | custom-call | tf_op jit(solution)/shard_map/pallas_call | solution.py:434
  97.7 0.0 copy-done
  97.7 0.0 copy-done.1
  97.7 16.1 %shard_map.120 = (bf16[32,2,48,1536]{3,2,1,0:T(8,128)(2,1)}, bf16[2,1536,512]{2,1,0:T(8,128)(2,1)}, bf16[2,1536,512]{2,1,0:T(8,128)(2,1)}, bf16[2,512,1536]{2,1,0:T(8,128)(2,1)}, f32[6,256]{1,0:T(8,128)}) custom-call(bf16[32,2,48,1024]{3,2,1,0:T(8,128)(2,1)} %get-tuple-element.14.dadb, bf16[2,1536,512]{2,1,0:T(8,128)(2,1)} %wg.1, bf16[2,1536,512]{2,1,0:T(8,128)(2,1)} %wu.1, ...), custom_call_target="tpu_custom_call" | custom-call | tf_op jit(solution)/shard_map/pallas_call | solution.py:540
Async XLA Ops:
  0.6 97.1 %copy-start = (s32[256,6]{0,1:T(8,128)S(1)}, s32[256,6]{0,1:T(8,128)}, u32[]{:S(2)}) copy-start(s32[256,6]{0,1:T(8,128)} %param.13) | copy-start | bytes 18436
  0.6 97.1 %copy-start.1 = (s32[256,6]{0,1:T(8,128)S(1)}, s32[256,6]{0,1:T(8,128)}, u32[]{:S(2)}) copy-start(s32[256,6]{0,1:T(8,128)} %param.14) | copy-start | bytes 18436

commit v6 on v5

--- a/solution.py
+++ b/solution.py
@@ -24,7 +24,7 @@
 
 ORIGIN_Y, ORIGIN_X = packed([b[0] for b in ORDER]), packed([b[1] for b in ORDER])
 QUARTERS = 4
-VMEM_A = 45 * 1024 * 1024 + 900 * 1024
+VMEM_A = 45 * 1024 * 1024 + 832 * 1024
 VMEM_B = 22 * 1024 * 1024
 UNIT_BLOCKS = 4
 STEP_BLOCKS = 2
@@ -54,8 +54,8 @@
 
 
 def expert_kernel(group_size, x_hbm, wg_hbm, wu_hbm, wd_hbm, dout_hbm, slots_ref, ids_ref, gates_ref,
-                  dadb_hbm, acc_gu, acc_d, back_hbm, pq_hbm, h_hbm,
-                  ag, rt, wgu, wd, xb, db, pq, hb, gsend, grecv,
+                  dadb_hbm, acc_gu, acc_d, grecv, pq_hbm, h_hbm,
+                  ag, rt, wgu, wd, xb, db, pq, hb, gsend,
                   w_sem, own_sem, x_sem, spill_sem, fill_sem, dadb_sem,
                   recv_sem, rrecv_sem, send_sem, rsend_sem,
                   srecv_sem, srrecv_sem, ssend_sem, srsend_sem, gsend_sem, grecv_sem):
@@ -171,9 +171,9 @@
     own.start()
     barrier = pltpu.get_barrier_semaphore()
 
-    @pl.loop(1, group_size)
-    def _(k):
-        pl.semaphore_signal(barrier, inc=1, device_id={'ep': lax.rem(me + k, group_size)}, device_id_type=MESH)
+    partners = [neighbour(dy, dx) for dy, dx in SENDS] + [sibling]
+    for to in partners:
+        pl.semaphore_signal(barrier, inc=1, device_id={'ep': to}, device_id_type=MESH)
 
     for c in w_copies[:2]:
         c.start()
@@ -187,7 +187,7 @@
     rt[0, 0, 0:top_k] = jnp.where(slots >= 0, ids_ref[...] * cap + slots, -1).astype(F32)
     rt[0, 0, 8:8 + top_k] = gates_ref[...]
     own.wait()
-    pl.semaphore_wait(barrier, group_size - 1)
+    pl.semaphore_wait(barrier, len(partners))
     for slot in range(3):
         issue(slot)
     for q in range(QUARTERS):
@@ -334,6 +334,19 @@
             for j in range(per_step):
                 dadb_copy(t, e, j).start()
 
+            @pl.when((t == 0) & (e == e_local - 1))
+            def _():
+                grecv[me] = gsend[0]
+
+            @pl.when(e == e_local - 1)
+            def _():
+                @pl.loop(jnp.where(t == 0, 1, 0), per_step)
+                def _(j):
+                    to = origin(t * STEP_BLOCKS + j // 2, lax.rem(j, 2))
+                    pltpu.make_async_remote_copy(
+                        src_ref=gsend.at[t * per_step + j], dst_ref=grecv.at[me], send_sem=gsend_sem,
+                        recv_sem=grecv_sem, device_id={'ep': to}, device_id_type=MESH).start()
+
             def weight_grads(rows, dy_rows):
                 @pl.loop(0, 2)
                 def _(m):
@@ -366,17 +379,6 @@
 
         on(AFTER, t)
 
-        @pl.when(t == 0)
-        def _():
-            grecv[me] = gsend[0]
-
-        @pl.loop(jnp.where(t == 0, 1, 0), per_step)
-        def _(j):
-            to = origin(t * STEP_BLOCKS + j // 2, lax.rem(j, 2))
-            pltpu.make_async_remote_copy(
-                src_ref=gsend.at[t * per_step + j], dst_ref=grecv.at[me], send_sem=gsend_sem,
-                recv_sem=grecv_sem, device_id={'ep': to}, device_id_type=MESH).start()
-
     def drain(ref, sem):
         pltpu.make_async_copy(ref, ref, sem).wait()
 
@@ -386,12 +388,9 @@
     drain(rt.at[0], srsend_sem)
     drain(gsend.at[pl.ds(0, group_size - 1)], gsend_sem)
     drain(grecv.at[pl.ds(0, group_size - 1)], grecv_sem)
-    back = pltpu.make_async_copy(grecv, back_hbm, own_sem)
-    back.start()
     for e in range(e_local):
         for j in range(per_step):
             dadb_copy(jnp.int32(steps - 1), e, j).wait()
-    back.wait()
 
 
 def run_experts(x_disp, w_gate, w_up, w_down, d_out, slots, ids, gates, group_size):
@@ -411,7 +410,7 @@
         jax.ShapeDtypeStruct((sources, e_local, cap, 2 * ffn), BF16),
         pltpu.VMEM((e_local, model, 2 * ffn), F32),
         pltpu.VMEM((e_local, ffn, model), F32),
-        jax.ShapeDtypeStruct((group_size, e_local, 1, tok), F32),
+        pltpu.VMEM((group_size, e_local, 1, tok), F32),
         jax.ShapeDtypeStruct((units, rows_u, 2 * ffn), F32),
         jax.ShapeDtypeStruct((units, rows_u, ffn), BF16),
     ]
@@ -425,7 +424,6 @@
         pltpu.VMEM((e_local, rows_u, 2 * ffn), F32),
         pltpu.VMEM((e_local, rows_u, ffn), BF16),
         pltpu.VMEM((group_size, e_local, 1, tok), F32),
-        pltpu.VMEM((group_size, e_local, 1, tok), F32),
         dma((3,)), dma, dma((e_local, per_unit)), dma((e_local, 2)), dma((e_local, 2)),
         dma((e_local, per_step)),
         dma((n_blocks, QUARTERS)), dma((n_blocks,)), dma, dma,
@@ -434,14 +432,14 @@
     return pl.pallas_call(
         functools.partial(expert_kernel, group_size),
         out_shape=out_shape, in_specs=[any_spec] * 5 + [vmem_spec] * 3,
-        out_specs=[any_spec, vmem_spec, vmem_spec, any_spec, any_spec, any_spec], scratch_shapes=scratch,
+        out_specs=[any_spec, vmem_spec, vmem_spec, vmem_spec, any_spec, any_spec], scratch_shapes=scratch,
         compiler_params=pltpu.CompilerParams(collective_id=0, has_side_effects=True, vmem_limit_bytes=VMEM_A),
     )(x_disp, w_gate, w_up, w_down, d_out, slots, ids, gates)
 
 
-def finish_kernel(group_size, chunk, dadb, wg, wu, back_hbm, acc_gu, acc_d, ids, slots,
+def finish_kernel(group_size, chunk, dadb, wg, wu, back, acc_gu, acc_d, ids, slots,
                   gx, g_gate, g_up, g_down, gate_out,
-                  wbuf, dbuf, obuf, st_g, st_u, st_d, back, w_sem, d_sem, o_sem, s_sem, b_sem):
+                  wbuf, dbuf, obuf, st_g, st_u, st_d, w_sem, d_sem, o_sem, s_sem):
     sources, e_local, cap, width = dadb.shape
     ffn = width // 2
     model = gx.shape[3]
@@ -480,42 +478,45 @@
         for c in weights(e):
             c.start()
 
-    back_copy = pltpu.make_async_copy(back_hbm, back, b_sem)
-    back_copy.start()
-
-    @pl.loop(0, chunks)
-    def _(c):
+    def cast(c):
         e, m, f, copies = staged(c)
-
-        @pl.when(lax.rem(c, per_e) == 0)
-        def _():
-            for w in weights(e):
-                w.wait()
-
-        load(c).wait()
-
-        @pl.when(c >= 2)
-        def _():
-            store(c - 2).wait()
-
-        slot, out_slot = lax.rem(c, depth), lax.rem(c, 2)
         st_g[e, m] = acc_gu[e, m, 0:ffn].astype(BF16)
         st_u[e, m] = acc_gu[e, m, ffn:width].astype(BF16)
         st_d[e, f] = acc_d[e, f].astype(BF16)
-        both = dbuf[slot].reshape(chunk * cap, width)
-        for n in range(model // 512):
-            rows = pl.ds(n * 512, 512)
-            out = lax.dot_general(both, wbuf[e, rows], NT, preferred_element_type=F32)
-            obuf[out_slot, :, :, rows] = out.astype(BF16).reshape(chunk, cap, 512)
-        store(c).start()
-        for s in copies:
+        return copies
+
+    @pl.loop(0, per_e)
+    def _(c):
+        for s in cast(c):
             s.start()
 
-        @pl.when(c + depth < chunks)
-        def _():
-            load(c + depth).start()
-
-    back_copy.wait()
+    for e in range(e_local):
+        for w in weights(e):
+            w.wait()
+
+        @pl.loop(e * per_e, (e + 1) * per_e)
+        def _(c, e=e):
+            load(c).wait()
+
+            @pl.when(c >= 2)
+            def _():
+                store(c - 2).wait()
+
+            slot, out_slot = lax.rem(c, depth), lax.rem(c, 2)
+            copies = cast(c + per_e) if e + 1 < e_local else []
+            both = dbuf[slot].reshape(chunk * cap, width)
+            for n in range(model // 512):
+                rows = pl.ds(n * 512, 512)
+                out = lax.dot_general(both, wbuf[e, rows], NT, preferred_element_type=F32)
+                obuf[out_slot, :, :, rows] = out.astype(BF16).reshape(chunk, cap, 512)
+            store(c).start()
+            for s in copies:
+                s.start()
+
+            @pl.when(c + depth < chunks)
+            def _():
+                load(c + depth).start()
+
     total = jnp.zeros(gate_out.shape, F32)
     for d in range(group_size):
         for e in range(e_local):
@@ -539,7 +540,7 @@
     vmem_spec = pl.BlockSpec(memory_space=pltpu.VMEM)
     return pl.pallas_call(
         functools.partial(finish_kernel, group_size, chunk),
-        in_specs=[any_spec] * 4 + [vmem_spec] * 4,
+        in_specs=[any_spec] * 3 + [vmem_spec] * 5,
         out_specs=[any_spec] * 4 + [vmem_spec],
         out_shape=[
             jax.ShapeDtypeStruct((sources, e_local, cap, model), BF16),
@@ -555,12 +556,11 @@
             pltpu.VMEM((e_local, model, ffn), BF16),
             pltpu.VMEM((e_local, model, ffn), BF16),
             pltpu.VMEM((e_local, ffn, model), BF16),
-            pltpu.VMEM(back.shape, F32),
-            dma((e_local, 2)), dma((3,)), dma((2,)), dma((e_local * sources // chunk, 3)), dma,
+            dma((e_local, 2)), dma((3,)), dma((2,)), dma((e_local * sources // chunk, 3)),
         ],
         compiler_params=pltpu.CompilerParams(vmem_limit_bytes=VMEM_B),
-    )(*[pltpu.with_memory_space_constraint(a, pltpu.HBM) for a in (dadb, w_gate, w_up, back)],
-      *[pltpu.with_memory_space_constraint(a, pltpu.VMEM) for a in (acc_gu, acc_d)], ids, slots)
+    )(*[pltpu.with_memory_space_constraint(a, pltpu.HBM) for a in (dadb, w_gate, w_up)],
+      *[pltpu.with_memory_space_constraint(a, pltpu.VMEM) for a in (back, acc_gu, acc_d)], ids, slots)
 
 
 def solution(mesh):

time: 114 us -> 112 us (0.982)
  Pallas kernels: 113 us -> 111 us
    pallas_call x1, Pallas kernels: 97 us -> 93.8 us  [run_experts(): pl.pallas_call(functools.partial(expert_kernel, group_size), out_shape=ou...]
    pallas_call x1, Pallas kernels: 16.1 us -> 17.3 us  [run_finish(): pl.pallas_call(functools.partial(finish_kernel, group_size, chunk), in_sp...]
where the time goes in v6:
time: 112 us
  Pallas kernels  111 us (99%)
    pallas_call x1, Pallas kernels, run_experts(): pl.pallas_call(functools.partial(expert_kernel, group_size), out_shape=ou...  93.8 us
    pallas_call x1, Pallas kernels, run_finish(): pl.pallas_call(functools.partial(finish_kernel, group_size, chunk), in_sp...  17.3 us

profile of v6, /device:TPU:97, one launch (start us, length us, event | category | flops | bytes accessed | tf_op | source)
XLA Modules:
  0.0 111.8 jit_solution(5059000873197536387)
XLA Ops:
  0.6 0.0 copy-start
  0.6 0.0 copy-start.1
  0.7 93.8 %shard_map.119 = (bf16[32,2,48,1024]{3,2,1,0:T(8,128)(2,1)}, f32[2,1536,1024]{2,1,0:T(8,128)S(1)}, f32[2,512,1536]{2,1,0:T(8,128)S(1)}, f32[32,2,1,256]{3,2,1,0:...) custom-call(bf16[32,2,48,1536]{3,2,1,0:T(8,128)(2,1)} %x_hbm.1, bf16[2,1536,512]{2,1,0:T(8,128)(2,1)} %wg.1, ...), custom_call_target="tpu_custom_call" | custom-call | tf_op jit(solution)/shard_map/pallas_call | solution.py:432
  94.5 0.0 copy-done
  94.5 0.0 copy-done.1
  94.5 17.3 %shard_map.120 = (bf16[32,2,48,1536]{3,2,1,0:T(8,128)(2,1)}, bf16[2,1536,512]{2,1,0:T(8,128)(2,1)}, bf16[2,1536,512]{2,1,0:T(8,128)(2,1)}, bf16[2,512,1536]{2,1,0:T(8,128)(2,1)}, f32[6,256]{1,0:T(8,128)}) custom-call(bf16[32,2,48,1024]{3,2,1,0:T(8,128)(2,1)} %get-tuple-element.14.dadb, bf16[2,1536,512]{2,1,0:T(8,128)(2,1)} %wg.1, bf16[2,1536,512]{2,1,0:T(8,128)(2,1)} %wu.1, ...), custom_call_target="tpu_custom_call" | custom-call | tf_op jit(solution)/shard_map/pallas_call | solution.py:541
Async XLA Ops:
  0.6 93.8 %copy-start = (s32[256,6]{0,1:T(8,128)S(1)}, s32[256,6]{0,1:T(8,128)}, u32[]{:S(2)}) copy-start(s32[256,6]{0,1:T(8,128)} %param.13) | copy-start | bytes 18436
  0.6 93.8 %copy-start.1 = (s32[256,6]{0,1:T(8,128)S(1)}, s32[256,6]{0,1:T(8,128)}, u32[]{:S(2)}) copy-start(s32[256,6]{0,1:T(8,128)} %param.14) | copy-start | bytes 18436

commit v7 on v6

--- a/solution.py
+++ b/solution.py
@@ -13,7 +13,7 @@
 MESH = pl.DeviceIdType.MESH
 
 ORDER = [(0, 0), (0, 1), (0, 3), (1, 0), (3, 0), (0, 2), (2, 0), (1, 1),
-         (1, 2), (3, 1), (1, 3), (3, 3), (3, 2), (2, 1), (2, 3), (2, 2)]
+         (1, 3), (3, 1), (3, 3), (1, 2), (2, 1), (2, 3), (3, 2), (2, 2)]
 PLACE = {block: place for place, block in enumerate(ORDER)}
 
 
@@ -28,22 +28,19 @@
 VMEM_B = 22 * 1024 * 1024
 UNIT_BLOCKS = 4
 STEP_BLOCKS = 2
-BEFORE = {0: (3,), 3: (7,), 4: (8, 9, 10), 6: (13,)}
-BETWEEN = {0: (4,), 1: (5,), 2: (6,), 4: (11,), 5: (12,)}
-AFTER = {6: (14,)}
+BEFORE = {0: (3,), 3: (7,), 4: (9,), 5: (11,), 6: (13,)}
+BETWEEN = {0: (4,), 1: (5,), 2: (6,), 3: (8,)}
+LATE = {4: (10,), 5: (12,), 6: (14,)}
 NT = (((1,), (1,)), ((), ()))
 TN = (((0,), (0,)), ((), ()))
 
 
 def send_lists():
-    own = [(0, 0, 0), (0, 0, 1), (0, 0, 2), (0, 0, 3), (0, 1, 0), (0, 1, 2)]
-    plus_x = own + [(1, 0, 2), (1, 0, 3), (3, 0, 2), (1, 1, 2), (3, 0, 3), (2, 0, 2),
-                    (3, 1, 2), (2, 0, 3), (2, 1, 2)]
-    swap = (2, 3, 0, 1)
     flip = (1, 0, 3, 2)
-    plus_y = [(ox, oy, swap[q]) for oy, ox, q in own]
-    plus_y += [(0, 1, 0), (0, 1, 1), (0, 2, 0), (0, 2, 1), (0, 3, 0), (0, 3, 1),
-               (1, 1, 0), (1, 3, 0), (1, 2, 0)]
+    plus_x = [(0, 0, 1), (0, 0, 0), (0, 0, 2), (0, 0, 3), (0, 1, 0), (0, 1, 2), (1, 0, 3), (1, 0, 2),
+              (3, 0, 2), (3, 0, 3), (2, 0, 2), (1, 1, 2), (2, 0, 3), (3, 1, 2), (2, 1, 2)]
+    plus_y = [(0, 0, 0), (0, 0, 3), (0, 0, 2), (0, 0, 1), (1, 0, 0), (1, 0, 2), (0, 1, 1), (0, 1, 0),
+              (0, 3, 1), (0, 3, 0), (0, 2, 0), (0, 2, 1), (1, 1, 0), (1, 3, 0), (1, 2, 0)]
     minus_x = [(oy, -ox % 4, flip[q]) for oy, ox, q in plus_x]
     minus_y = [(-oy % 4, ox, flip[q]) for oy, ox, q in plus_y]
     return {(0, 1): plus_x, (0, 3): minus_x, (1, 0): plus_y, (3, 0): minus_y}
@@ -178,7 +175,7 @@
     for c in w_copies[:2]:
         c.start()
     for e in range(e_local):
-        for c in unit_x(0, e):
+        for c in unit_x(1, e):
             c.start()
     w_copies[2].start()
     top_k = slots_ref.shape[0]
@@ -211,13 +208,14 @@
 
     @pl.loop(0, units * e_local)
     def _(u):
-        g, e = u // e_local, lax.rem(u, e_local)
+        turn, e = u // e_local, lax.rem(u, e_local)
+        g = lax.rem(turn + 1, units)
         for c in unit_x(g, e):
             c.wait()
 
         @pl.when(u >= e_local)
         def _():
-            for c in spill_copies(u - e_local, e):
+            for c in spill_copies(g * e_local + e, e):
                 c.wait()
 
         @pl.loop(0, ft_count)
@@ -233,12 +231,11 @@
             pq[e, :, lo] = b * sg * (1.0 + a * (1.0 - sg))
             pq[e, :, hi] = silu
 
-        for c in spill_copies(u, e):
-            c.start()
-
-        @pl.when(g + 1 < units)
+        @pl.when(turn + 1 < units)
         def _():
-            for c in unit_x(g + 1, e):
+            for c in spill_copies(g * e_local + e, e):
+                c.start()
+            for c in unit_x(lax.rem(turn + 2, units), e):
                 c.start()
 
         for k, at in ((0, 2), (1, 4), (2, 6)):
@@ -246,12 +243,6 @@
             def _(k=k):
                 service(k)
 
-    for e in range(e_local):
-        for c in spill_copies((units - 1) * e_local + e, e):
-            c.wait()
-    for e in range(e_local):
-        for c in unit_fill(0, e):
-            c.start()
     w_copies[2].wait()
 
     def hits(r, p, e):
@@ -278,13 +269,17 @@
         here = pl.ds(half, rows_s)
         dy_here = pl.ds(pl.multiple_of(rows_s + half, rows_s), rows_s)
 
-        @pl.loop(0, STEP_BLOCKS)
-        def _(i):
-            p = t * STEP_BLOCKS + i
-            for q in range(QUARTERS):
-                sib_copy(p, q).wait_recv()
-            sib_route(p).wait_recv()
-            for r in range(2):
+        @pl.loop(0, 2)
+        def _(r):
+            @pl.when(r == 1)
+            def _():
+                for i in range(STEP_BLOCKS):
+                    for q in range(QUARTERS):
+                        sib_copy(t * STEP_BLOCKS + i, q).wait_recv()
+                    sib_route(t * STEP_BLOCKS + i).wait_recv()
+
+            for i in range(STEP_BLOCKS):
+                p = t * STEP_BLOCKS + i
                 picks, gates = [], []
                 for e in range(e_local):
                     slot, gate = hits(r, p, e)
@@ -299,11 +294,12 @@
                     for e in range(e_local):
                         d_e = d[e * cap:(e + 1) * cap]
                         db[e, pl.ds(row, cap), cols] = d_e.astype(BF16)
-                        db[e, pl.ds(pl.multiple_of(rows_s + half + row, cap), cap), cols] = (d_e * gates[e]).astype(BF16)
+                        db[e, pl.ds(pl.multiple_of(rows_s + half + row, cap), cap), cols] = (
+                            d_e * gates[e]).astype(BF16)
 
         @pl.loop(0, e_local)
         def _(e):
-            @pl.when(odd == 0)
+            @pl.when((odd == 0) & (t > 0))
             def _():
                 for c in unit_fill(t // 2, e):
                     c.wait()
@@ -361,6 +357,12 @@
                     acc_d[e, :, cols] += lax.dot_general(
                         hb[e, rows, :], db[e, dy_rows, cols], TN, preferred_element_type=F32)
 
+            for step, slots in LATE.items():
+                @pl.when((t == step) & (e == e_local - 1))
+                def _(slots=slots):
+                    for k in slots:
+                        service(k)
+
             @pl.when((odd == 1) & (t < steps - 2))
             def _():
                 weight_grads(pl.ds(0, rows_u), pl.ds(rows_s, rows_u))
@@ -377,7 +379,6 @@
                     for k in slots:
                         service(k)
 
-        on(AFTER, t)
 
     def drain(ref, sem):
         pltpu.make_async_copy(ref, ref, sem).wait()
@@ -485,11 +486,6 @@
         st_d[e, f] = acc_d[e, f].astype(BF16)
         return copies
 
-    @pl.loop(0, per_e)
-    def _(c):
-        for s in cast(c):
-            s.start()
-
     for e in range(e_local):
         for w in weights(e):
             w.wait()
@@ -503,7 +499,7 @@
                 store(c - 2).wait()
 
             slot, out_slot = lax.rem(c, depth), lax.rem(c, 2)
-            copies = cast(c + per_e) if e + 1 < e_local else []
+            copies = cast(c)
             both = dbuf[slot].reshape(chunk * cap, width)
             for n in range(model // 512):
                 rows = pl.ds(n * 512, 512)

time: 112 us -> 110 us (0.982)
  Pallas kernels: 111 us -> 109 us
    pallas_call x1, Pallas kernels: 17.3 us -> 16.1 us  [run_finish(): pl.pallas_call(functools.partial(finish_kernel, group_size, chunk), in_sp...]
where the time goes in v7:
time: 110 us
  Pallas kernels  109 us (99%)
    pallas_call x1, Pallas kernels, run_experts(): pl.pallas_call(functools.partial(expert_kernel, group_size), out_shape=ou...  92.8 us
    pallas_call x1, Pallas kernels, run_finish(): pl.pallas_call(functools.partial(finish_kernel, group_size, chunk), in_sp...  16.1 us

profile of v7, /device:TPU:97, one launch (start us, length us, event | category | flops | bytes accessed | tf_op | source)
XLA Modules:
  0.0 109.6 jit_solution(5612656198017338771)
XLA Ops:
  0.6 0.0 copy-start
  0.6 0.0 copy-start.1
  0.7 92.8 %shard_map.119 = (bf16[32,2,48,1024]{3,2,1,0:T(8,128)(2,1)}, f32[2,1536,1024]{2,1,0:T(8,128)S(1)}, f32[2,512,1536]{2,1,0:T(8,128)S(1)}, f32[32,2,1,256]{3,2,1,0:...) custom-call(bf16[32,2,48,1536]{3,2,1,0:T(8,128)(2,1)} %x_hbm.1, bf16[2,1536,512]{2,1,0:T(8,128)(2,1)} %wg.1, ...), custom_call_target="tpu_custom_call" | custom-call | tf_op jit(solution)/shard_map/pallas_call | solution.py:433
  93.5 0.0 copy-done
  93.5 0.0 copy-done.1
  93.5 16.1 %shard_map.120 = (bf16[32,2,48,1536]{3,2,1,0:T(8,128)(2,1)}, bf16[2,1536,512]{2,1,0:T(8,128)(2,1)}, bf16[2,1536,512]{2,1,0:T(8,128)(2,1)}, bf16[2,512,1536]{2,1,0:T(8,128)(2,1)}, f32[6,256]{1,0:T(8,128)}) custom-call(bf16[32,2,48,1024]{3,2,1,0:T(8,128)(2,1)} %get-tuple-element.14.dadb, bf16[2,1536,512]{2,1,0:T(8,128)(2,1)} %wg.1, bf16[2,1536,512]{2,1,0:T(8,128)(2,1)} %wu.1, ...), custom_call_target="tpu_custom_call" | custom-call | tf_op jit(solution)/shard_map/pallas_call | solution.py:537
Async XLA Ops:
  0.6 92.8 %copy-start = (s32[256,6]{0,1:T(8,128)S(1)}, s32[256,6]{0,1:T(8,128)}, u32[]{:S(2)}) copy-start(s32[256,6]{0,1:T(8,128)} %param.13) | copy-start | bytes 18436
  0.6 92.8 %copy-start.1 = (s32[256,6]{0,1:T(8,128)S(1)}, s32[256,6]{0,1:T(8,128)}, u32[]{:S(2)}) copy-start(s32[256,6]{0,1:T(8,128)} %param.14) | copy-start | bytes 18436

commit v8 on v7

--- a/solution.py
+++ b/solution.py
@@ -363,15 +363,18 @@
                     for k in slots:
                         service(k)
 
-            @pl.when((odd == 1) & (t < steps - 2))
+            @pl.when(t == 1)
             def _():
                 weight_grads(pl.ds(0, rows_u), pl.ds(rows_s, rows_u))
+
+            @pl.when(t > 1)
+            def _():
+                weight_grads(here, dy_here)
+
+            @pl.when((odd == 1) & (t < steps - 1))
+            def _():
                 for c in unit_fill(t // 2 + 1, e):
                     c.start()
-
-            @pl.when(t >= steps - 2)
-            def _():
-                weight_grads(here, dy_here)
 
             for step, slots in BETWEEN.items():
                 @pl.when((t == step) & (e == 0))
@@ -459,9 +462,12 @@
         return pltpu.make_async_copy(
             obuf.at[slot], gx.at[pl.ds(lax.rem(c, per_e) * chunk, chunk), c // per_e], o_sem.at[slot])
 
-    def weights(e):
-        return [pltpu.make_async_copy(wg.at[e], wbuf.at[e, :, pl.ds(0, ffn)], w_sem.at[e, 0]),
-                pltpu.make_async_copy(wu.at[e], wbuf.at[e, :, pl.ds(ffn, ffn)], w_sem.at[e, 1])]
+    tiles = [pl.ds(n * 512, 512) for n in range(model // 512)]
+
+    def weights(e, n):
+        rows = tiles[n]
+        return [pltpu.make_async_copy(wg.at[e, rows], wbuf.at[e, rows, pl.ds(0, ffn)], w_sem.at[e, n, 0]),
+                pltpu.make_async_copy(wu.at[e, rows], wbuf.at[e, rows, pl.ds(ffn, ffn)], w_sem.at[e, n, 1])]
 
     def staged(c):
         e, i = c // per_e, lax.rem(c, per_e)
@@ -471,13 +477,14 @@
                          pltpu.make_async_copy(st_u.at[e, m], g_up.at[e, m], s_sem.at[c, 1]),
                          pltpu.make_async_copy(st_d.at[e, f], g_down.at[e, f], s_sem.at[c, 2])]
 
-    for c in weights(0):
-        c.start()
-    for k in range(depth):
-        load(jnp.int32(k)).start()
-    for e in range(1, e_local):
-        for c in weights(e):
-            c.start()
+    load(jnp.int32(0)).start()
+    for e in range(e_local):
+        for n in range(len(tiles)):
+            for c in weights(e, n):
+                c.start()
+        if e == 0:
+            for k in range(1, depth):
+                load(jnp.int32(k)).start()
 
     def cast(c):
         e, m, f, copies = staged(c)
@@ -486,32 +493,36 @@
         st_d[e, f] = acc_d[e, f].astype(BF16)
         return copies
 
+    def product(c, e, wait):
+        load(c).wait()
+
+        @pl.when(c >= 2)
+        def _():
+            store(c - 2).wait()
+
+        slot, out_slot = lax.rem(c, depth), lax.rem(c, 2)
+        copies = cast(c)
+        both = dbuf[slot].reshape(chunk * cap, width)
+        for n, rows in enumerate(tiles):
+            if wait:
+                for w in weights(e, n):
+                    w.wait()
+            out = lax.dot_general(both, wbuf[e, rows], NT, preferred_element_type=F32)
+            obuf[out_slot, :, :, rows] = out.astype(BF16).reshape(chunk, cap, 512)
+        store(c).start()
+        for s in copies:
+            s.start()
+
+        @pl.when(c + depth < chunks)
+        def _():
+            load(c + depth).start()
+
     for e in range(e_local):
-        for w in weights(e):
-            w.wait()
-
-        @pl.loop(e * per_e, (e + 1) * per_e)
+        product(jnp.int32(e * per_e), e, True)
+
+        @pl.loop(e * per_e + 1, (e + 1) * per_e)
         def _(c, e=e):
-            load(c).wait()
-
-            @pl.when(c >= 2)
-            def _():
-                store(c - 2).wait()
-
-            slot, out_slot = lax.rem(c, depth), lax.rem(c, 2)
-            copies = cast(c)
-            both = dbuf[slot].reshape(chunk * cap, width)
-            for n in range(model // 512):
-                rows = pl.ds(n * 512, 512)
-                out = lax.dot_general(both, wbuf[e, rows], NT, preferred_element_type=F32)
-                obuf[out_slot, :, :, rows] = out.astype(BF16).reshape(chunk, cap, 512)
-            store(c).start()
-            for s in copies:
-                s.start()
-
-            @pl.when(c + depth < chunks)
-            def _():
-                load(c + depth).start()
+            product(c, e, False)
 
     total = jnp.zeros(gate_out.shape, F32)
     for d in range(group_size):
@@ -552,7 +563,7 @@
             pltpu.VMEM((e_local, model, ffn), BF16),
             pltpu.VMEM((e_local, model, ffn), BF16),
             pltpu.VMEM((e_local, ffn, model), BF16),
-            dma((e_local, 2)), dma((3,)), dma((2,)), dma((e_local * sources // chunk, 3)),
+            dma((e_local, model // 512, 2)), dma((3,)), dma((2,)), dma((e_local * sources // chunk, 3)),
         ],
         compiler_params=pltpu.CompilerParams(vmem_limit_bytes=VMEM_B),
     )(*[pltpu.with_memory_space_constraint(a, pltpu.HBM) for a in (dadb, w_gate, w_up)],

time: 110 us -> 112 us (1.018)
  Pallas kernels: 109 us -> 111 us
    pallas_call x1, Pallas kernels: 16.1 us -> 17.7 us  [run_finish(): pl.pallas_call(functools.partial(finish_kernel, group_size, chunk), in_sp...]
where the time goes in v8:
time: 112 us
  Pallas kernels  111 us (99%)
    pallas_call x1, Pallas kernels, run_experts(): pl.pallas_call(functools.partial(expert_kernel, group_size), out_shape=ou...  93.4 us
    pallas_call x1, Pallas kernels, run_finish(): pl.pallas_call(functools.partial(finish_kernel, group_size, chunk), in_sp...  17.7 us

profile of v8, /device:TPU:97, one launch (start us, length us, event | category | flops | bytes accessed | tf_op | source)
XLA Modules:
  0.0 111.8 jit_solution(13215928696526727705)
XLA Ops:
  0.6 0.0 copy-start
  0.6 0.0 copy-start.1
  0.7 93.4 %shard_map.119 = (bf16[32,2,48,1024]{3,2,1,0:T(8,128)(2,1)}, f32[2,1536,1024]{2,1,0:T(8,128)S(1)}, f32[2,512,1536]{2,1,0:T(8,128)S(1)}, f32[32,2,1,256]{3,2,1,0:...) custom-call(bf16[32,2,48,1536]{3,2,1,0:T(8,128)(2,1)} %x_hbm.1, bf16[2,1536,512]{2,1,0:T(8,128)(2,1)} %wg.1, ...), custom_call_target="tpu_custom_call" | custom-call | tf_op jit(solution)/shard_map/pallas_call | solution.py:436
  94.1 0.0 copy-done
  94.1 0.0 copy-done.1
  94.1 17.7 %shard_map.120 = (bf16[32,2,48,1536]{3,2,1,0:T(8,128)(2,1)}, bf16[2,1536,512]{2,1,0:T(8,128)(2,1)}, bf16[2,1536,512]{2,1,0:T(8,128)(2,1)}, bf16[2,512,1536]{2,1,0:T(8,128)(2,1)}, f32[6,256]{1,0:T(8,128)}) custom-call(bf16[32,2,48,1024]{3,2,1,0:T(8,128)(2,1)} %get-tuple-element.14.dadb, bf16[2,1536,512]{2,1,0:T(8,128)(2,1)} %wg.1, bf16[2,1536,512]{2,1,0:T(8,128)(2,1)} %wu.1, ...), custom_call_target="tpu_custom_call" | custom-call | tf_op jit(solution)/shard_map/pallas_call | solution.py:548
Async XLA Ops:
  0.6 93.5 %copy-start = (s32[256,6]{0,1:T(8,128)S(1)}, s32[256,6]{0,1:T(8,128)}, u32[]{:S(2)}) copy-start(s32[256,6]{0,1:T(8,128)} %param.13) | copy-start | bytes 18436
  0.6 93.5 %copy-start.1 = (s32[256,6]{0,1:T(8,128)S(1)}, s32[256,6]{0,1:T(8,128)}, u32[]{:S(2)}) copy-start(s32[256,6]{0,1:T(8,128)} %param.14) | copy-start | bytes 18436

commit v9 on v8

--- a/solution.py
+++ b/solution.py
@@ -363,13 +363,9 @@
                     for k in slots:
                         service(k)
 
-            @pl.when(t == 1)
+            @pl.when(odd == 1)
             def _():
                 weight_grads(pl.ds(0, rows_u), pl.ds(rows_s, rows_u))
-
-            @pl.when(t > 1)
-            def _():
-                weight_grads(here, dy_here)
 
             @pl.when((odd == 1) & (t < steps - 1))
             def _():
@@ -462,12 +458,9 @@
         return pltpu.make_async_copy(
             obuf.at[slot], gx.at[pl.ds(lax.rem(c, per_e) * chunk, chunk), c // per_e], o_sem.at[slot])
 
-    tiles = [pl.ds(n * 512, 512) for n in range(model // 512)]
-
-    def weights(e, n):
-        rows = tiles[n]
-        return [pltpu.make_async_copy(wg.at[e, rows], wbuf.at[e, rows, pl.ds(0, ffn)], w_sem.at[e, n, 0]),
-                pltpu.make_async_copy(wu.at[e, rows], wbuf.at[e, rows, pl.ds(ffn, ffn)], w_sem.at[e, n, 1])]
+    def weights(e):
+        return [pltpu.make_async_copy(wg.at[e], wbuf.at[e, :, pl.ds(0, ffn)], w_sem.at[e, 0]),
+                pltpu.make_async_copy(wu.at[e], wbuf.at[e, :, pl.ds(ffn, ffn)], w_sem.at[e, 1])]
 
     def staged(c):
         e, i = c // per_e, lax.rem(c, per_e)
@@ -477,14 +470,13 @@
                          pltpu.make_async_copy(st_u.at[e, m], g_up.at[e, m], s_sem.at[c, 1]),
                          pltpu.make_async_copy(st_d.at[e, f], g_down.at[e, f], s_sem.at[c, 2])]
 
-    load(jnp.int32(0)).start()
-    for e in range(e_local):
-        for n in range(len(tiles)):
-            for c in weights(e, n):
-                c.start()
-        if e == 0:
-            for k in range(1, depth):
-                load(jnp.int32(k)).start()
+    for c in weights(0):
+        c.start()
+    for k in range(depth):
+        load(jnp.int32(k)).start()
+    for e in range(1, e_local):
+        for c in weights(e):
+            c.start()
 
     def cast(c):
         e, m, f, copies = staged(c)
@@ -493,7 +485,15 @@
         st_d[e, f] = acc_d[e, f].astype(BF16)
         return copies
 
-    def product(c, e, wait):
+    @pl.loop(0, chunks)
+    def _(c):
+        e = c // per_e
+
+        @pl.when(lax.rem(c, per_e) == 0)
+        def _():
+            for w in weights(e):
+                w.wait()
+
         load(c).wait()
 
         @pl.when(c >= 2)
@@ -503,10 +503,8 @@
         slot, out_slot = lax.rem(c, depth), lax.rem(c, 2)
         copies = cast(c)
         both = dbuf[slot].reshape(chunk * cap, width)
-        for n, rows in enumerate(tiles):
-            if wait:
-                for w in weights(e, n):
-                    w.wait()
+        for n in range(model // 512):
+            rows = pl.ds(n * 512, 512)
             out = lax.dot_general(both, wbuf[e, rows], NT, preferred_element_type=F32)
             obuf[out_slot, :, :, rows] = out.astype(BF16).reshape(chunk, cap, 512)
         store(c).start()
@@ -516,13 +514,6 @@
         @pl.when(c + depth < chunks)
         def _():
             load(c + depth).start()
-
-    for e in range(e_local):
-        product(jnp.int32(e * per_e), e, True)
-
-        @pl.loop(e * per_e + 1, (e + 1) * per_e)
-        def _(c, e=e):
-            product(c, e, False)
 
     total = jnp.zeros(gate_out.shape, F32)
     for d in range(group_size):
@@ -563,7 +554,7 @@
             pltpu.VMEM((e_local, model, ffn), BF16),
             pltpu.VMEM((e_local, model, ffn), BF16),
             pltpu.VMEM((e_local, ffn, model), BF16),
-            dma((e_local, model // 512, 2)), dma((3,)), dma((2,)), dma((e_local * sources // chunk, 3)),
+            dma((e_local, 2)), dma((3,)), dma((2,)), dma((e_local * sources // chunk, 3)),
         ],
         compiler_params=pltpu.CompilerParams(vmem_limit_bytes=VMEM_B),
     )(*[pltpu.with_memory_space_constraint(a, pltpu.HBM) for a in (dadb, w_gate, w_up)],

time: 112 us -> 108 us (0.964)
  Pallas kernels: 111 us -> 107 us
    pallas_call x1, Pallas kernels: 93.4 us -> 91.3 us  [run_experts(): pl.pallas_call(functools.partial(expert_kernel, group_size), out_shape=ou...]
    pallas_call x1, Pallas kernels: 17.7 us -> 16.1 us  [run_finish(): pl.pallas_call(functools.partial(finish_kernel, group_size, chunk), in_sp...]
where the time goes in v9:
time: 108 us
  Pallas kernels  107 us (99%)
    pallas_call x1, Pallas kernels, run_experts(): pl.pallas_call(functools.partial(expert_kernel, group_size), out_shape=ou...  91.3 us
    pallas_call x1, Pallas kernels, run_finish(): pl.pallas_call(functools.partial(finish_kernel, group_size, chunk), in_sp...  16.1 us

profile of v9, /device:TPU:97, one launch (start us, length us, event | category | flops | bytes accessed | tf_op | source)
XLA Modules:
  0.0 108.1 jit_solution(10467116938239080711)
XLA Ops:
  0.6 0.0 copy-start
  0.6 0.0 copy-start.1
  0.7 91.3 %shard_map.119 = (bf16[32,2,48,1024]{3,2,1,0:T(8,128)(2,1)}, f32[2,1536,1024]{2,1,0:T(8,128)S(1)}, f32[2,512,1536]{2,1,0:T(8,128)S(1)}, f32[32,2,1,256]{3,2,1,0:...) custom-call(bf16[32,2,48,1536]{3,2,1,0:T(8,128)(2,1)} %x_hbm.1, bf16[2,1536,512]{2,1,0:T(8,128)(2,1)} %wg.1, ...), custom_call_target="tpu_custom_call" | custom-call | tf_op jit(solution)/shard_map/pallas_call | solution.py:432
  91.9 0.0 copy-done
  91.9 0.0 copy-done.1
  91.9 16.1 %shard_map.120 = (bf16[32,2,48,1536]{3,2,1,0:T(8,128)(2,1)}, bf16[2,1536,512]{2,1,0:T(8,128)(2,1)}, bf16[2,1536,512]{2,1,0:T(8,128)(2,1)}, bf16[2,512,1536]{2,1,0:T(8,128)(2,1)}, f32[6,256]{1,0:T(8,128)}) custom-call(bf16[32,2,48,1024]{3,2,1,0:T(8,128)(2,1)} %get-tuple-element.14.dadb, bf16[2,1536,512]{2,1,0:T(8,128)(2,1)} %wg.1, bf16[2,1536,512]{2,1,0:T(8,128)(2,1)} %wu.1, ...), custom_call_target="tpu_custom_call" | custom-call | tf_op jit(solution)/shard_map/pallas_call | solution.py:539
Async XLA Ops:
  0.6 91.3 %copy-start = (s32[256,6]{0,1:T(8,128)S(1)}, s32[256,6]{0,1:T(8,128)}, u32[]{:S(2)}) copy-start(s32[256,6]{0,1:T(8,128)} %param.13) | copy-start | bytes 18436
  0.6 91.3 %copy-start.1 = (s32[256,6]{0,1:T(8,128)S(1)}, s32[256,6]{0,1:T(8,128)}, u32[]{:S(2)}) copy-start(s32[256,6]{0,1:T(8,128)} %param.14) | copy-start | bytes 18436
